TPU v7x, 16 devices: a 4x2x1 block of a 4x4x8 slice. The times are simulated.
16 devices in a mesh: rep: 2 (over y, z), dp: 8 (over x, core).
Axes of the slice: x: 4, y: 2, z: 1, core: 2. Of those that a mesh axis runs over, the one named last changes fastest.
The devices are a block of a 4x4x8 slice.
Arguments:
- g_w_gate: bfloat16 [16, 2, 1024, 2816], P(('rep', 'dp')), parts along dimension 0
- g_w_up: bfloat16 [16, 2, 1024, 2816], P(('rep', 'dp')), parts along dimension 0
- g_w_down: bfloat16 [16, 2, 2816, 1024], P(('rep', 'dp')), parts along dimension 0
- w_gate: bfloat16 [2, 1024, 2816], replicated
- w_up: bfloat16 [2, 1024, 2816], replicated
- w_down: bfloat16 [2, 2816, 1024], replicated
- m_w_gate: float32 [2, 1024, 2816], P(None, 'dp')
- m_w_up: float32 [2, 1024, 2816], P(None, 'dp')
- m_w_down: float32 [2, 2816, 1024], P(None, 'dp')
- v_w_gate: float32 [2, 1024, 2816], P(None, 'dp')
- v_w_up: float32 [2, 1024, 2816], P(None, 'dp')
- v_w_down: float32 [2, 2816, 1024], P(None, 'dp')
Outputs:
- output 1: bfloat16 [4, 1024, 2816], P('rep'), parts along dimension 0
- output 2: bfloat16 [4, 1024, 2816], P('rep'), parts along dimension 0
- output 3: bfloat16 [4, 2816, 1024], P('rep'), parts along dimension 0
- output 4: float32 [4, 1024, 2816], P('rep', 'dp'), parts along dimension 0
- output 5: float32 [4, 1024, 2816], P('rep', 'dp'), parts along dimension 0
- output 6: float32 [4, 2816, 1024], P('rep', 'dp'), parts along dimension 0
- output 7: float32 [4, 1024, 2816], P('rep', 'dp'), parts along dimension 0
- output 8: float32 [4, 1024, 2816], P('rep', 'dp'), parts along dimension 0
- output 9: float32 [4, 2816, 1024], P('rep', 'dp'), parts along dimension 0
There are 2 independent parts. A program takes and returns all parts, laid end to end along the dimension named above; an argument that names none is the same for every part.
All inputs are finite; a program needn't handle non-finite values.
Results may differ from a plain program's by a relative error of at most 0.022.
Values are sent between devices in bfloat16 or wider.
A program may use at most 768 MiB of HBM per device.

v0:
```python
import jax
import jax.numpy as jnp
from jax import lax
from jax.sharding import PartitionSpec as P


def adamw(w, m, v, g):
    m = 0.9 * m + 0.1 * g
    v = 0.95 * v + 0.05 * g * g
    step = m * lax.rsqrt(v + 1e-8) + 0.1 * w
    return (w - 0.02 * step).astype(jnp.bfloat16), m, v


def clipped(gradients, sum_of_squares, count):
    factor = jnp.minimum(1.0, 0.5 * lax.rsqrt(sum_of_squares / count + 1e-30))
    return [g * factor for g in gradients]


def solution(mesh):
    def step(*arrays):
        terms, weights, m, v = (arrays[i : i + 3] for i in (0, 3, 6, 9))
        gradients = [lax.psum_scatter(t[0], "dp", scatter_dimension=1, tiled=True).astype(jnp.float32) for t in terms]
        squares = lax.psum(sum(jnp.sum(g * g) for g in gradients), "dp")
        gradients = clipped(gradients, squares, lax.psum(1, "dp") * sum(g.size for g in gradients))
        me = lax.axis_index("dp")
        own = [lax.dynamic_slice_in_dim(w, me * one.shape[1], one.shape[1], 1).astype(jnp.float32) for w, one in zip(weights, m, strict=True)]
        new = [adamw(w, m, v, g) for w, m, v, g in zip(own, m, v, gradients, strict=True)]
        whole = [lax.all_gather(one[0], "dp", axis=1, tiled=True) for one in new]
        return (*whole, *(one[1] for one in new), *(one[2] for one in new))

    all_of, cut = P(None, None, None), P(None, "dp", None)
    return jax.shard_map(
        step,
        mesh=mesh,
        in_specs=(P(("rep", "dp"), None, None, None),) * 3 + (all_of,) * 3 + (cut,) * 6,
        out_specs=(P("rep", None, None),) * 3 + (P("rep", "dp", None),) * 6,
        check_vma=False,
    )
```

profile of v0, /device:TPU:113, one launch (start us, length us, event | category | flops | bytes accessed | tf_op | source)
XLA Modules:
  0.0 444.1 jit_solution(14709896009177031959)
XLA Ops:
  7.2 0.1 reduce-scatter.4.cloned.1.call-start
  7.3 0.7 reduce-scatter.4.cloned.1.call-update
  8.0 0.1 reduce-scatter.6.cloned.1.call-start
  8.1 0.7 reduce-scatter.6.cloned.1.call-update
  8.8 0.1 reduce-scatter.8.cloned.1.call-start
  8.9 0.7 reduce-scatter.8.cloned.1.call-update
  9.6 0.1 all-gather.8.cloned.1.call-start
  9.7 66.5 %reduce-scatter.4.cloned.1.call-done = bf16[2,128,2816]{2,1,0:T(8,128)(2,1)} async-done(((bf16[2,1024,2816]{2,1,0:T(8,128)(2,1)}), bf16[2,128,2816]{2,1,0:T(8,128)(2,1)}) %reduce-scatter.4.cloned.1.call-update) | async-done | bytes 1441808 | tf_op jit(solution)/shard_map/reduce_scatter | solution.py:22
  76.2 2.7 fusion.9
  78.9 62.7 %reduce-scatter.6.cloned.1.call-done = bf16[2,128,2816]{2,1,0:T(8,128)(2,1)} async-done(((bf16[2,1024,2816]{2,1,0:T(8,128)(2,1)}), bf16[2,128,2816]{2,1,0:T(8,128)(2,1)}) %reduce-scatter.6.cloned.1.call-update) | async-done | bytes 1441808 | tf_op jit(solution)/shard_map/reduce_scatter | solution.py:22
  141.6 2.7 fusion.10
  145.6 61.4 %reduce-scatter.8.cloned.1.call-done = bf16[2,352,1024]{2,1,0:T(8,128)(2,1)} async-done(((bf16[2,2816,1024]{2,1,0:T(8,128)(2,1)}), bf16[2,352,1024]{2,1,0:T(8,128)(2,1)}) %reduce-scatter.8.cloned.1.call-update) | async-done | bytes 1441808 | tf_op jit(solution)/shard_map/reduce_scatter | solution.py:22
  207.0 2.7 fusion.11
  210.3 13.4 %psum.7 = f32[]{:T(128)} all-reduce(f32[]{:T(128)S(6)} %add.65), channel_id=1, replica_groups=mesh['rep'=2,'dp'=8] {'dp'}, use_global_device_ids=true, to_apply=%region_6.0 | all-reduce | flops 1 | bytes 8 | tf_op jit(solution)/shard_map/psum | solution.py:23
  224.5 0.0 copy-start.2
  224.5 7.7 %fusion.17 = (bf16[2,352,1024]{2,1,0:T(8,128)(2,1)}, f32[2,352,1024]{2,1,0:T(8,128)}, f32[2,352,1024]{2,1,0:T(8,128)}) fusion(bf16[2,2816,1024]{2,1,0:T(8,128)(2,1)} %param.17, s32[]{:T(128)S(6)} %select_n.8, f32[]{:T(128)S(6)} %min_shard_map.3, bf16[2,352,1024]{2,1,0:T(8,128)(2,1)} %reduce-scatter.8.cloned.1.call-done, f32[2,352,1024]{2,1,0:T(8,128)} %param.23, ...), kind=kLoop, calls=%fused_computation.32 | loop fusion | flops 12255232 | bytes 15859720 | tf_op jit(solution)/shard_map/convert_element_type | solution.py:11
  232.2 0.1 all-gather.8.cloned.1.call-update
  232.3 0.1 all-gather.4.cloned.1.call-start
  232.4 0.0 copy-done.2
  232.4 7.0 %fusion.8 = (bf16[2,128,2816]{2,1,0:T(8,128)(2,1)}, f32[2,128,2816]{2,1,0:T(8,128)}, f32[2,128,2816]{2,1,0:T(8,128)}) fusion(bf16[2,1024,2816]{2,1,0:T(8,128)(2,1)} %param.15, s32[]{:T(128)S(6)} %select_n.7, f32[]{:T(128)S(6)} %min_shard_map.3, bf16[2,128,2816]{2,1,0:T(8,128)(2,1)S(1)} %copy-done.2, f32[2,128,2816]{2,1,0:T(8,128)} %param.21, ...), kind=kLoop, calls=%fused_computation.23 | loop fusion | flops 12255232 | bytes 15859720 | tf_op jit(solution)/shard_map/convert_element_type | solution.py:11
  239.3 0.1 all-gather.4.cloned.1.call-update
  239.4 0.1 all-gather.6.cloned.1.call-start
  239.5 6.9 %fusion.14 = (bf16[2,128,2816]{2,1,0:T(8,128)(2,1)}, f32[2,128,2816]{2,1,0:T(8,128)}, f32[2,128,2816]{2,1,0:T(8,128)}) fusion(bf16[2,1024,2816]{2,1,0:T(8,128)(2,1)} %param.16, s32[]{:T(128)S(6)} %select_n.7, f32[]{:T(128)S(6)} %min_shard_map.3, bf16[2,128,2816]{2,1,0:T(8,128)(2,1)S(1)} %copy-done.1, f32[2,128,2816]{2,1,0:T(8,128)} %param.22, ...), kind=kLoop, calls=%fused_computation.29 | loop fusion | flops 12255232 | bytes 15859720 | tf_op jit(solution)/shard_map/convert_element_type | solution.py:11
  246.4 0.1 all-gather.6.cloned.1.call-update
  246.4 44.4 %all-gather.8.cloned.1.call-done = bf16[2,2816,1024]{2,1,0:T(8,128)(2,1)} async-done(((bf16[2,352,1024]{2,1,0:T(8,128)(2,1)}), bf16[2,2816,1024]{2,1,0:T(8,128)(2,1)}) %all-gather.8.cloned.1.call-update) | async-done | bytes 11534352 | tf_op jit(solution)/shard_map/all_gather | solution.py:28
  290.9 61.2 %all-gather.4.cloned.1.call-done = bf16[2,1024,2816]{2,1,0:T(8,128)(2,1)} async-done(((bf16[2,128,2816]{2,1,0:T(8,128)(2,1)}), bf16[2,1024,2816]{2,1,0:T(8,128)(2,1)}) %all-gather.4.cloned.1.call-update) | async-done | bytes 11534352 | tf_op jit(solution)/shard_map/all_gather | solution.py:28
  352.0 61.2 %all-gather.6.cloned.1.call-done = bf16[2,1024,2816]{2,1,0:T(8,128)(2,1)} async-done(((bf16[2,128,2816]{2,1,0:T(8,128)(2,1)}), bf16[2,1024,2816]{2,1,0:T(8,128)(2,1)}) %all-gather.6.cloned.1.call-update) | async-done | bytes 11534352 | tf_op jit(solution)/shard_map/all_gather | solution.py:28
  413.2 11.7 %copy.24 = bf16[2,1024,2816]{2,1,0:T(8,128)(2,1)} copy(bf16[2,1024,2816]{2,1,0:T(8,128)(2,1)} %all-gather.4.cloned.1.call-done) | data formatting | bytes 23068672
  424.9 5.8 %copy.25 = bf16[2,1024,2816]{2,1,0:T(8,128)(2,1)} copy(bf16[2,1024,2816]{2,1,0:T(8,128)(2,1)S(1)} %copy-done) | data formatting | bytes 23068672
  430.7 0.8 slice-done.1
  431.5 1.2 slice-done.2
  432.8 4.4 copy.26
  (9 shorter events, 0.0 us)
Async XLA Ops:
  7.2 69.0 %reduce-scatter.4.cloned.1.call-start = ((), (), s32[]{:S(2)}) async-start(), calls=%async_computation.3 | async-start | bytes 12976128 | tf_op jit(solution)/shard_map/reduce_scatter | solution.py:22
  8.0 133.6 %reduce-scatter.6.cloned.1.call-start = ((), (), s32[]{:S(2)}) async-start(), calls=%async_computation.4 | async-start | bytes 12976128 | tf_op jit(solution)/shard_map/reduce_scatter | solution.py:22
  8.8 198.2 %reduce-scatter.8.cloned.1.call-start = ((), (), s32[]{:S(2)}) async-start(), calls=%async_computation.5 | async-start | bytes 12976128 | tf_op jit(solution)/shard_map/reduce_scatter | solution.py:22
  9.6 281.3 %all-gather.8.cloned.1.call-start = ((), (), s32[]{:S(2)}) async-start(), calls=%async_computation.8 | async-start | bytes 12976128 | tf_op jit(solution)/shard_map/all_gather | solution.py:28
  224.5 7.9 %copy-start.2 = (bf16[2,128,2816]{2,1,0:T(8,128)(2,1)S(1)}, bf16[2,128,2816]{2,1,0:T(8,128)(2,1)}, u32[]{:S(2)}) copy-start(bf16[2,128,2816]{2,1,0:T(8,128)(2,1)} %reduce-scatter.4.cloned.1.call-done) | copy-start | bytes 4325380
  232.3 119.8 %all-gather.4.cloned.1.call-start = ((), (), s32[]{:S(2)}) async-start(), calls=%async_computation.6 | async-start | bytes 12976128 | tf_op jit(solution)/shard_map/all_gather | solution.py:28
  232.4 7.1 %copy-start.1 = (bf16[2,128,2816]{2,1,0:T(8,128)(2,1)S(1)}, bf16[2,128,2816]{2,1,0:T(8,128)(2,1)}, u32[]{:S(2)}) copy-start(bf16[2,128,2816]{2,1,0:T(8,128)(2,1)} %reduce-scatter.6.cloned.1.call-done) | copy-start | bytes 4325380
  239.4 173.8 %all-gather.6.cloned.1.call-start = ((), (), s32[]{:S(2)}) async-start(), calls=%async_computation.7 | async-start | bytes 12976128 | tf_op jit(solution)/shard_map/all_gather | solution.py:28
  413.2 11.7 %copy-start = (bf16[2,1024,2816]{2,1,0:T(8,128)(2,1)S(1)}, bf16[2,1024,2816]{2,1,0:T(8,128)(2,1)}, u32[]{:S(2)}) copy-start(bf16[2,1024,2816]{2,1,0:T(8,128)(2,1)} %all-gather.6.cloned.1.call-done) | copy-start | bytes 34603012
  413.2 17.5 %slice-start = ((s8[11534336]{0:T(1024)(128)(4,1)}), s8[4194304]{0:T(1024)(128)(4,1)S(1)}, s32[]{:S(2)}) async-start(s8[11534336]{0:T(1024)(128)(4,1)} %bitcast.6), calls=%async_computation.9 | async-start | bytes 8388608
  413.2 18.3 %slice-start.1 = ((s8[11534336]{0:T(1024)(128)(4,1)}), s8[4194304]{0:T(1024)(128)(4,1)S(1)}, s32[]{:S(2)}) async-start(s8[11534336]{0:T(1024)(128)(4,1)} %bitcast.6), calls=%async_computation.10 | async-start | bytes 8388608
  424.9 7.9 %slice-start.2 = ((s8[11534336]{0:T(1024)(128)(4,1)}), s8[3145728]{0:T(1024)(128)(4,1)S(1)}, s32[]{:S(2)}) async-start(s8[11534336]{0:T(1024)(128)(4,1)} %bitcast.6), calls=%async_computation.11 | async-start | bytes 6291456
Sparse Core Ops, SparseCore 0:
  10.3 65.8 reduce-scatter.3
  78.5 63.0 reduce-scatter.5
  143.9 63.0 reduce-scatter.7
  232.4 58.4 all-gather.7
  292.9 59.1 all-gather.3
  354.0 59.1 all-gather.5
where the time goes:
time: 444 us
  waiting for transfers between devices  360 us (81%)
  other arithmetic  29.7 us (7%)
  local copies, waits for them, and re-layouts  24 us (5%)
  between operations  16.8 us (4%)
  blocking collectives  13.4 us (3%)
    reduce_scatter x3, waiting for transfers between devices, step(): lax.psum_scatter(t[0], 'dp', scatter_dimension=1, tiled=True)  191 us
    all_gather x3, waiting for transfers between devices, step(): whole = [lax.all_gather(one[0], 'dp', axis=1, tiled=True) for one in new]  167 us
    unnamed x15, local copies, waits for them, and re-layouts  24 us
    convert_element_type x3, other arithmetic, adamw(): return ((w - 0.02 * step).astype(jnp.bfloat16), m, v)  21.6 us
    psum x1, blocking collectives, step(): squares = lax.psum(sum((jnp.sum(g * g) for g in gradients)), 'dp')  13.4 us
  transfers between devices with their start and end apart: 6, of which 6 were waited for; matrix products, arithmetic and copies ran while one was open for 4% of the time, Pallas kernels for 0%

commit v1 on v0

v1 whole, which is shorter than its diff:
```python
import functools

import jax
import jax.numpy as jnp
from jax import lax
from jax.experimental import pallas as pl
from jax.experimental.pallas import tpu as pltpu
from jax.sharding import PartitionSpec as P

AXIS = "dp"
CORES = 2
AHEAD = 6
GROUP = 16
A, B, C, OWN = 0, 2, 4, 6


def adamw(w, m, v, g):
    m = 0.9 * m + 0.1 * g
    v = 0.95 * v + 0.05 * g * g
    step = m * lax.rsqrt(v + 1e-8) + 0.1 * w
    return (w - 0.02 * step).astype(jnp.bfloat16), m, v


class Places:
    def __init__(self, n, shapes):
        self.n = n
        self.layers = shapes[0][0]
        self.half = [rows // n // 2 for _, rows, _ in shapes]
        self.piece = [(h, cols) for h, (_, _, cols) in zip(self.half, shapes)]
        self.count = len(shapes) * self.layers
        self.kinds = sorted(set(self.piece), key=self.piece.index)
        self.members = [[p for p in range(self.count) if self.piece[p // self.layers] == k] for k in self.kinds]

    def scratch(self, slots, dtype):
        return [pltpu.VMEM((len(m) * slots, *k), dtype) for m, k in zip(self.members, self.kinds)]

    def at(self, buffers, slots, p, slot):
        kind = self.kinds.index(self.piece[p // self.layers])
        return buffers[kind].at[self.members[kind].index(p) * slots + slot]

    def rows(self, refs, p, block, half):
        w = p // self.layers
        start = pl.multiple_of((block * 2 + half) * self.half[w], GROUP)
        return refs[w].at[p % self.layers, pl.ds(start, self.half[w]), :]

    def own(self, refs, p, half):
        w = p // self.layers
        return refs[w].at[p % self.layers, pl.ds(half * self.half[w], self.half[w]), :]


def exchange(places, tail, count, *refs):
    nk = len(places.kinds)
    names = (3, 3, 3, 3, 3, 3, 1, 2 * len(tail), nk, nk, nk, nk, nk, nk, nk, 1, 1, 1, 1, 1, 1, 1, 1, 1)
    parts, i = [], 0
    for size in names:
        parts.append(refs[i : i + size])
        i += size
    g, w, m, v, whole, summed, (factor_ref,), tails = parts[:8]
    own, par, got, mm, vv, ww, acc = parts[8:15]
    (sq,), (own_sem,), (par_send,), (par_recv,), (snd,), (rcv,), (mvw_sem,), (sq_send,), (sq_recv,) = parts[15:]

    n, at = places.n, places.at
    chips = n // CORES
    me = lax.axis_index(AXIS)
    core, chip = lax.rem(me, CORES), lax.div(me, CORES)
    away = lambda k, core: lax.rem(chip + (k + chips), chips) * CORES + core
    partner = away(0, 1 - core)
    sign = (1, -1)
    beside = [away(s, core) for s in sign]

    def remote(src, dst, send, recv, device):
        return pltpu.make_async_remote_copy(
            src_ref=src, dst_ref=dst, send_sem=send, recv_sem=recv, device_id={AXIS: device}, device_id_type=pl.DeviceIdType.MESH
        )

    def place(kind):
        i = kind % 2
        if kind < B:
            return 2, 1 - i, i
        if kind < C:
            return sign[i], i, 2 + i
        if kind < OWN:
            return sign[i], 1 - i, i
        return 0, i, 3 - i

    spots = range(places.count)
    steps = [(k + i, p) for k in (A, B, C) for p in spots for i in range(2)] + [(OWN + h, p) for p in spots for h in (1, 0)]

    def load(kind, p):
        to, half, slot = place(kind)
        return pltpu.make_async_copy(places.rows(g, p, away(to, core), half), at(own, 4, p, slot), own_sem.at[p, slot])

    def give(kind, p):
        to, half, _ = place(kind)
        return remote(places.rows(g, p, away(to, 1 - core), half), at(par, 8, p, kind), par_send.at[p, kind], par_recv.at[p, kind], partner)

    def send(kind, p):
        slot = place(kind)[2]
        return remote(at(own, 4, p, slot), at(got, 6, p, kind), snd.at[p, kind], rcv.at[p, kind], beside[kind % 2])

    def start_load(t):
        kind, p = steps[t]
        if kind >= C:
            send(kind - C if kind < OWN else B + 1 - (kind - OWN), p).wait_send()
        load(kind, p).start()

    def add_up(kind, p):
        out = at(own, 4, p, place(kind)[2])
        terms = [out, at(par, 8, p, kind)]
        if C <= kind < OWN:
            terms.append(at(got, 6, p, kind - C))
        if kind >= OWN:
            i = 1 - (kind - OWN)
            terms += [at(got, 6, p, C + i), at(got, 6, p, B + 1 - i)]
        squares = acc[places.kinds.index(places.piece[p // places.layers])]

        def body(r, carry):
            rows = pl.ds(pl.multiple_of(r * GROUP, GROUP), GROUP)
            total = terms[0][rows, :].astype(jnp.float32)
            for one in terms[1:]:
                total = total + one[rows, :].astype(jnp.float32)
            total = total.astype(jnp.bfloat16)
            out[rows, :] = total
            if kind >= OWN:
                total = total.astype(jnp.float32)
                squares[...] += total * total
            return carry

        lax.fori_loop(0, places.half[p // places.layers] // GROUP, body, 0)

    def moments(p, h):
        return [
            pltpu.make_async_copy(places.own(m, p, h), at(mm, 2, p, h), mvw_sem.at[p, h, 0]),
            pltpu.make_async_copy(places.own(v, p, h), at(vv, 2, p, h), mvw_sem.at[p, h, 1]),
            pltpu.make_async_copy(places.rows(w, p, me, h), at(ww, 2, p, h), mvw_sem.at[p, h, 2]),
        ]

    for t in range(AHEAD):
        start_load(t)
    barrier = pltpu.get_barrier_semaphore()
    for o in range(1, n):
        pl.semaphore_signal(barrier, inc=1, device_id={AXIS: lax.rem(me + o, n)}, device_id_type=pl.DeviceIdType.MESH)
    pl.semaphore_wait(barrier, n - 1)
    for t in range(AHEAD):
        give(*steps[t]).start()
    for one in acc:
        one[...] = jnp.zeros_like(one)

    for t, (kind, p) in enumerate(steps):
        if t + AHEAD < len(steps):
            give(*steps[t + AHEAD]).start()
        load(kind, p).wait()
        give(kind, p).wait_recv()
        if C <= kind < OWN:
            send(kind - C, p).wait_recv()
        if kind >= OWN:
            i = 1 - (kind - OWN)
            send(B + 1 - i, p).wait_recv()
            send(C + i, p).wait_recv()
        add_up(kind, p)
        if kind < OWN:
            send(kind, p).start()
        if t + AHEAD < len(steps):
            start_load(t + AHEAD)
        if t == 2 * places.count:
            for q in spots:
                for h in range(2):
                    for copy in moments(q, h):
                        copy.start()

    sq[me] = jnp.full(sq.shape[1:], sum(jnp.sum(one[...]) for one in acc), jnp.float32)

    def tell(o, device):
        return remote(sq.at[device], sq.at[device], sq_send.at[o], sq_recv.at[o], lax.rem(me + o, n))

    for o in range(1, n):
        tell(o, me).start()
    for p in spots:
        for i in range(2):
            send(C + i, p).wait_send()
        for kind in range(8):
            give(kind, p).wait_send()
    for o in range(1, n):
        tell(o, lax.rem(me + (n - o), n)).wait_recv()
    for o in range(1, n):
        tell(o, me).wait_send()
    total = sq[0]
    for d in range(1, n):
        total = total + sq[d]
    factor_ref[...] = jnp.minimum(1.0, 0.5 * lax.rsqrt(total / count + 1e-30))

    def ahead(i, p, h):
        k = 2 * i + h
        return remote(at(ww, 2, p, h), places.rows(whole, p, me, h), snd.at[p, k], rcv.at[p, k], beside[i])

    def ahead_came(i, p, h):
        k = 2 * i + h
        here = places.rows(whole, p, away(-sign[i], core), h)
        return remote(here, here, snd.at[p, k], rcv.at[p, k], beside[i])

    def onward(i, p):
        here = places.rows(whole, p, away(-sign[i], core), 1 - i)
        return remote(here, here, snd.at[p, 4 + i], rcv.at[p, 4 + i], beside[i])

    def onward_came(i, p):
        here = places.rows(whole, p, away(2, core), 1 - i)
        return remote(here, here, snd.at[p, 4 + i], rcv.at[p, 4 + i], beside[i])

    def across(k, p):
        if k < 4:
            here = places.rows(whole, p, away(-sign[k // 2], core), k % 2)
        elif k < 6:
            here = places.rows(whole, p, away(2, core), 1 - (k - 4))
        else:
            here = places.rows(whole, p, me, k - 6)
        src = here if k < 6 else at(ww, 2, p, k - 6)
        return remote(src, here, par_send.at[p, k], par_recv.at[p, k], partner)

    def across_came(k, p):
        if k < 4:
            here = places.rows(whole, p, away(-sign[k // 2], 1 - core), k % 2)
        elif k < 6:
            here = places.rows(whole, p, away(2, 1 - core), 1 - (k - 4))
        else:
            here = places.rows(whole, p, partner, k - 6)
        return remote(here, here, par_send.at[p, k], par_recv.at[p, k], partner)

    def keep(p, h):
        return [
            pltpu.make_async_copy(at(ww, 2, p, h), places.rows(whole, p, me, h), own_sem.at[p, h]),
            pltpu.make_async_copy(at(own, 4, p, 3 - h), places.own(summed, p, h), own_sem.at[p, 2 + h]),
        ]

    def hand(p, h):
        return pltpu.make_async_copy(at(ww, 2, p, h), tails[2 * tail.index(p) + h], mvw_sem.at[p, h, 0])

    def update(p, h):
        for copy in moments(p, h):
            copy.wait()
        gs, ms, vs, ws = at(own, 4, p, 3 - h), at(mm, 2, p, h), at(vv, 2, p, h), at(ww, 2, p, h)

        def body(r, carry):
            rows = pl.ds(pl.multiple_of(r * GROUP, GROUP), GROUP)
            grad = gs[rows, :].astype(jnp.float32) * factor_ref[0:1, 0:1]
            ws[rows, :] = adamw(ws[rows, :].astype(jnp.float32), ms[rows, :], vs[rows, :], grad)[0]
            return carry

        lax.fori_loop(0, places.half[p // places.layers] // GROUP, body, 0)

    for p in spots:
        for h in (1, 0):
            update(p, h)
            ahead(1 - h, p, h).start()
            across(6 + h, p).start()
            for copy in keep(p, h):
                copy.start()
            if p in tail:
                hand(p, h).start()
    later = [p for p in spots if p not in tail]
    for p in later:
        for h in (0, 1):
            ahead(h, p, h).start()
    for p in spots:
        for i in range(2):
            ahead_came(i, p, 1 - i).wait_recv()
            onward(i, p).start()
            across(2 * i + 1 - i, p).start()
    for p in later:
        for i in range(2):
            ahead_came(i, p, i).wait_recv()
            across(2 * i + i, p).start()
    for p in spots:
        for i in range(2):
            onward_came(i, p).wait_recv()
            across(4 + i, p).start()
    for p in spots:
        for h in range(2):
            ahead(1 - h, p, h).wait_send()
            if p in later:
                ahead(h, p, h).wait_send()
            onward(h, p).wait_send()
            for copy in keep(p, h):
                copy.wait()
            if p in tail:
                hand(p, h).wait()
        for k in range(8):
            if k in (0, 3) and p in tail:
                continue
            across(k, p).wait_send()
            across_came(k, p).wait_recv()


def gather_new(terms, weights, m, v, n, tail):
    shapes = [w.shape for w in weights]
    places = Places(n, shapes)
    count = float(sum(w.size for w in weights))
    anywhere, vmem = pl.BlockSpec(memory_space=pl.ANY), pl.BlockSpec(memory_space=pltpu.VMEM)
    out = [jax.ShapeDtypeStruct(s, jnp.bfloat16) for s in shapes]
    out += [jax.ShapeDtypeStruct(one.shape, jnp.bfloat16) for one in m]
    out += [jax.ShapeDtypeStruct((8, 128), jnp.float32)]
    out += [jax.ShapeDtypeStruct(places.piece[p // places.layers], jnp.bfloat16) for p in tail for _ in range(2)]
    dma = pltpu.SemaphoreType.DMA
    half = jnp.bfloat16
    scratch = [
        *places.scratch(4, half), *places.scratch(8, half), *places.scratch(6, half),
        *places.scratch(2, jnp.float32), *places.scratch(2, jnp.float32), *places.scratch(2, half),
        *(pltpu.VMEM((GROUP, k[1]), jnp.float32) for k in places.kinds),
        pltpu.VMEM((n, 8, 128), jnp.float32),
        dma((places.count, 4)), dma((places.count, 8)), dma((places.count, 8)), dma((places.count, 6)), dma((places.count, 6)),
        dma((places.count, 2, 3)), dma((n,)), dma((n,)),
    ]
    got = pl.pallas_call(
        functools.partial(exchange, places, tail, count),
        out_shape=out,
        in_specs=[anywhere] * 12,
        out_specs=[anywhere] * 6 + [vmem] + [anywhere] * (2 * len(tail)),
        scratch_shapes=scratch,
        compiler_params=pltpu.CompilerParams(collective_id=0, has_side_effects=True, vmem_limit_bytes=66 * 1000 * 1000),
        name="exchange",
    )(*terms, *weights, *m, *v)
    return got[:3], got[3:6], got[6], got[7:]


def solution(mesh):
    n = mesh.shape[AXIS]

    def step(*arrays):
        terms, weights, m, v = (arrays[i : i + 3] for i in (0, 3, 6, 9))
        whole, summed, factor, _ = gather_new([t[0] for t in terms], weights, m, v, n, [])
        grads = [g.astype(jnp.float32) * factor[0, 0] for g in summed]
        new_m = [0.9 * a + 0.1 * g for a, g in zip(m, grads)]
        new_v = [0.95 * a + 0.05 * g * g for a, g in zip(v, grads)]
        return (*whole, *new_m, *new_v)

    all_of, cut = P(None, None, None), P(None, AXIS, None)
    return jax.shard_map(
        step,
        mesh=mesh,
        in_specs=(P(("rep", AXIS), None, None, None),) * 3 + (all_of,) * 3 + (cut,) * 6,
        out_specs=(P("rep", None, None),) * 3 + (P("rep", AXIS, None),) * 6,
        check_vma=False,
    )
```

time: 444 us -> 339 us (0.76)
  waiting for transfers between devices: 360 us -> 0 us
  Pallas kernels: 0 us -> 299 us
  between operations: 16.8 us -> 0.69 us
  blocking collectives: 13.4 us -> 0 us
  other arithmetic: 29.7 us -> 18.5 us
    pallas_call x0 -> x1, Pallas kernels: none -> 299 us  [gather_new(): pl.pallas_call(functools.partial(exchange, places, tail, count), out_shap...]
    reduce_scatter x3 -> x0, waiting for transfers between devices: 191 us -> none  [step(): lax.psum_scatter(t[0], 'dp', scatter_dimension=1, tiled=True)]
    all_gather x3 -> x0, waiting for transfers between devices: 167 us -> none  [step(): whole = [lax.all_gather(one[0], 'dp', axis=1, tiled=True) for one in new]]
    convert_element_type x3 -> x0, other arithmetic: 21.6 us -> none  [adamw(): return ((w - 0.02 * step).astype(jnp.bfloat16), m, v)]
    add x0 -> x2, other arithmetic: none -> 18.5 us  [step(): new_v = [0.95 * a + 0.05 * g * g for a, g in zip(v, grads)]]
    psum x1 -> x0, blocking collectives: 13.4 us -> none  [step(): squares = lax.psum(sum((jnp.sum(g * g) for g in gradients)), 'dp')]
    reduce_sum x3 -> x0, other arithmetic: 8.12 us -> none  [step(): squares = lax.psum(sum((jnp.sum(g * g) for g in gradients)), 'dp')]
    unnamed x15 -> x21, local copies, waits for them, and re-layouts: 24 us -> 19.8 us
  transfers between devices with their start and end apart: 6 -> 0, of which waited for: 6 -> 0; matrix products, arithmetic and copies ran while one was open for 4% -> 0% of each run, Pallas kernels for 0% -> 0%
where the time goes in v1:
time: 339 us
  Pallas kernels  299 us (88%)
  local copies, waits for them, and re-layouts  20.9 us (6%)
  other arithmetic  18.5 us (5%)
    pallas_call x1, Pallas kernels, gather_new(): pl.pallas_call(functools.partial(exchange, places, tail, count), out_shap...  299 us
    unnamed x21, local copies, waits for them, and re-layouts  19.8 us
    add x2, other arithmetic, step(): new_v = [0.95 * a + 0.05 * g * g for a, g in zip(v, grads)]  18.5 us

profile of v1, /device:TPU:113, one launch (start us, length us, event | category | flops | bytes accessed | tf_op | source)
XLA Modules:
  0.0 339.0 jit_solution(2322048753614102031)
XLA Ops:
  0.6 298.8 %exchange.1 = (bf16[2,1024,2816]{2,1,0:T(8,128)(2,1)}, bf16[2,1024,2816]{2,1,0:T(8,128)(2,1)}, bf16[2,2816,1024]{2,1,0:T(8,128)(2,1)}, bf16[2,128,2816]{2,1,0:T(...) custom-call(bf16[2,1024,2816]{2,1,0:T(8,128)(2,1)} %bitcast.8, ...), custom_call_target="tpu_custom_call" | custom-call | tf_op jit(solution)/shard_map/exchange/pallas_call | solution.py:312
  299.4 1.2 slice.2
  300.6 0.0 copy-start.1
  300.6 0.0 copy-start.2
  300.6 11.5 %fusion = (f32[2,128,2816]{2,1,0:T(8,128)}, f32[2,128,2816]{2,1,0:T(8,128)}, f32[2,128,2816]{2,1,0:T(8,128)}, f32[2,128,2816]{2,1,0:T(8,128)}) fusion(f32[2,128,2816]{2,1,0:T(8,128)} %refs_9_.1, bf16[2,128,2816]{2,1,0:T(8,128)(2,1)} %get-tuple-element.19, f32[]{:T(128)} %bitcast.3, f32[2,128,2816]{2,1,0:T(8,128)} %refs_6_.1, ...), kind=kLoop, calls=%fused_computation.3 | loop fusion | flops 12976128 | bytes 25952260 | tf_op jit(solution)/shard_map/add | solution.py:332
  312.2 0.0 copy-start
  312.2 0.0 copy-done.1
  312.2 0.0 copy-done.2
  312.2 0.0 slice-start.3
  312.2 0.0 slice-start.4
  312.2 7.0 %fusion.2 = (f32[2,352,1024]{2,1,0:T(8,128)}, f32[2,352,1024]{2,1,0:T(8,128)}) fusion(f32[2,352,1024]{2,1,0:T(8,128)} %refs_11_.1, bf16[2,352,1024]{2,1,0:T(8,128)(2,1)S(1)} %copy-done.2, f32[]{:T(128)} %bitcast.3, f32[2,352,1024]{2,1,0:T(8,128)S(1)} %copy-done.1), kind=kLoop, calls=%fused_computation.5 | loop fusion | flops 6488064 | bytes 12976132 | tf_op jit(solution)/shard_map/add | solution.py:332
  319.2 0.0 copy-done
  319.2 0.0 slice-start.5
  319.2 0.0 slice-start
  319.2 0.0 slice-start.1
  319.2 5.8 %copy.24 = bf16[2,1024,2816]{2,1,0:T(8,128)(2,1)} copy(bf16[2,1024,2816]{2,1,0:T(8,128)(2,1)S(1)} %copy-done) | data formatting | bytes 23068672
  325.1 0.0 slice-done.3
  325.1 0.0 slice-done.4
  325.1 2.0 slice-done.5
  327.0 0.0 slice-start.2
  327.0 5.8 %copy.25 = bf16[2,1024,2816]{2,1,0:T(8,128)(2,1)} copy(bf16[2,1024,2816]{2,1,0:T(8,128)(2,1)S(1)} %bitcast.7) | data formatting | bytes 23068672
  332.9 0.0 slice-done
  332.9 0.0 slice-done.1
  332.9 1.6 slice-done.2
  334.5 4.4 %copy.26 = bf16[2,2816,1024]{2,1,0:T(8,128)(2,1)} copy(bf16[2,2816,1024]{2,1,0:T(8,128)(2,1)S(1)} %bitcast.5) | data formatting | bytes 23068672
  (2 shorter events, 0.0 us)
Async XLA Ops:
  300.6 11.5 %copy-start.1 = (f32[2,352,1024]{2,1,0:T(8,128)S(1)}, f32[2,352,1024]{2,1,0:T(8,128)}, u32[]{:S(2)}) copy-start(f32[2,352,1024]{2,1,0:T(8,128)} %refs_8_.1) | copy-start | bytes 8650756
  300.6 11.5 %copy-start.2 = (bf16[2,352,1024]{2,1,0:T(8,128)(2,1)S(1)}, bf16[2,352,1024]{2,1,0:T(8,128)(2,1)}, u32[]{:S(2)}) copy-start(bf16[2,352,1024]{2,1,0:T(8,128)(2,1)} %get-tuple-element.22) | copy-start | bytes 4325380
  312.2 7.1 %copy-start = (bf16[2,1024,2816]{2,1,0:T(8,128)(2,1)S(1)}, bf16[2,1024,2816]{2,1,0:T(8,128)(2,1)}, u32[]{:S(2)}) copy-start(bf16[2,1024,2816]{2,1,0:T(8,128)(2,1)} %get-tuple-element.40) | copy-start | bytes 34603012
  312.2 12.9 %slice-start.3 = ((s8[11534336]{0:T(1024)(128)(4,1)}), s8[4194304]{0:T(1024)(128)(4,1)S(1)}, s32[]{:S(2)}) async-start(s8[11534336]{0:T(1024)(128)(4,1)} %bitcast.6), calls=%async_computation.3 | async-start | bytes 8388608
  312.2 12.9 %slice-start.4 = ((s8[11534336]{0:T(1024)(128)(4,1)}), s8[3145728]{0:T(1024)(128)(4,1)S(1)}, s32[]{:S(2)}) async-start(s8[11534336]{0:T(1024)(128)(4,1)} %bitcast.6), calls=%async_computation.4 | async-start | bytes 6291456
  319.2 7.8 %slice-start.5 = ((s8[11534336]{0:T(1024)(128)(4,1)}), s8[4194304]{0:T(1024)(128)(4,1)S(1)}, s32[]{:S(2)}) async-start(s8[11534336]{0:T(1024)(128)(4,1)} %bitcast.6), calls=%async_computation.5 | async-start | bytes 8388608
  319.2 13.7 %slice-start = ((s8[11534336]{0:T(1024)(128)(4,1)}), s8[4194304]{0:T(1024)(128)(4,1)S(1)}, s32[]{:S(2)}) async-start(s8[11534336]{0:T(1024)(128)(4,1)} %bitcast.4), calls=%async_computation | async-start | bytes 8388608
  319.2 13.7 %slice-start.1 = ((s8[11534336]{0:T(1024)(128)(4,1)}), s8[4194304]{0:T(1024)(128)(4,1)S(1)}, s32[]{:S(2)}) async-start(s8[11534336]{0:T(1024)(128)(4,1)} %bitcast.4), calls=%async_computation.1 | async-start | bytes 8388608
  327.0 7.5 %slice-start.2 = ((s8[11534336]{0:T(1024)(128)(4,1)}), s8[3145728]{0:T(1024)(128)(4,1)S(1)}, s32[]{:S(2)}) async-start(s8[11534336]{0:T(1024)(128)(4,1)} %bitcast.4), calls=%async_computation.2 | async-start | bytes 6291456

commit v2 on v1

--- a/solution.py
+++ b/solution.py
@@ -7,10 +7,13 @@
 from jax.experimental.pallas import tpu as pltpu
 from jax.sharding import PartitionSpec as P
 
+
 AXIS = "dp"
 CORES = 2
 AHEAD = 6
 GROUP = 16
+FIRST = 2
+SLOTS, DEPTH = 24, 12
 A, B, C, OWN = 0, 2, 4, 6
 
 
@@ -34,9 +37,13 @@
     def scratch(self, slots, dtype):
         return [pltpu.VMEM((len(m) * slots, *k), dtype) for m, k in zip(self.members, self.kinds)]
 
+    def spot(self, p):
+        kind = self.kinds.index(self.piece[p // self.layers])
+        return kind, self.members[kind].index(p)
+
     def at(self, buffers, slots, p, slot):
-        kind = self.kinds.index(self.piece[p // self.layers])
-        return buffers[kind].at[self.members[kind].index(p) * slots + slot]
+        kind, j = self.spot(p)
+        return buffers[kind].at[j * slots + slot]
 
     def rows(self, refs, p, block, half):
         w = p // self.layers
@@ -50,12 +57,12 @@
 
 def exchange(places, tail, count, *refs):
     nk = len(places.kinds)
-    names = (3, 3, 3, 3, 3, 3, 1, 2 * len(tail), nk, nk, nk, nk, nk, nk, nk, 1, 1, 1, 1, 1, 1, 1, 1, 1)
+    names = (3, 3, 3, 3, 3, 3, 1, 2 * nk + 1, nk, nk, nk, nk, nk, nk, nk, 1, 1, 1, 1, 1, 1, 1, 1, 1)
     parts, i = [], 0
     for size in names:
         parts.append(refs[i : i + size])
         i += size
-    g, w, m, v, whole, summed, (factor_ref,), tails = parts[:8]
+    g, w, m, v, whole, summed, (factor_ref,), (*tails, last) = parts[:8]
     own, par, got, mm, vv, ww, acc = parts[8:15]
     (sq,), (own_sem,), (par_send,), (par_recv,), (snd,), (rcv,), (mvw_sem,), (sq_send,), (sq_recv,) = parts[15:]
 
@@ -138,19 +145,20 @@
     for t in range(AHEAD):
         start_load(t)
     barrier = pltpu.get_barrier_semaphore()
-    for o in range(1, n):
-        pl.semaphore_signal(barrier, inc=1, device_id={AXIS: lax.rem(me + o, n)}, device_id_type=pl.DeviceIdType.MESH)
-    pl.semaphore_wait(barrier, n - 1)
-    for t in range(AHEAD):
+    for device in (partner, *beside):
+        pl.semaphore_signal(barrier, inc=1, device_id={AXIS: device}, device_id_type=pl.DeviceIdType.MESH)
+    pl.semaphore_wait(barrier, 3)
+    for t in range(FIRST):
         give(*steps[t]).start()
     for one in acc:
         one[...] = jnp.zeros_like(one)
 
+    given = lambda t: min(FIRST + 2 * t, t + AHEAD, len(steps))
     for t, (kind, p) in enumerate(steps):
-        if t + AHEAD < len(steps):
-            give(*steps[t + AHEAD]).start()
         load(kind, p).wait()
         give(kind, p).wait_recv()
+        for ahead in range(given(t), given(t + 1)):
+            give(*steps[ahead]).start()
         if C <= kind < OWN:
             send(kind - C, p).wait_recv()
         if kind >= OWN:
@@ -200,10 +208,11 @@
 
     def onward(i, p):
         here = places.rows(whole, p, away(-sign[i], core), 1 - i)
-        return remote(here, here, snd.at[p, 4 + i], rcv.at[p, 4 + i], beside[i])
+        there = last.at[i] if p == places.count - 1 else here
+        return remote(here, there, snd.at[p, 4 + i], rcv.at[p, 4 + i], beside[i])
 
     def onward_came(i, p):
-        here = places.rows(whole, p, away(2, core), 1 - i)
+        here = last.at[i] if p == places.count - 1 else places.rows(whole, p, away(2, core), 1 - i)
         return remote(here, here, snd.at[p, 4 + i], rcv.at[p, 4 + i], beside[i])
 
     def across(k, p):
@@ -232,7 +241,8 @@
         ]
 
     def hand(p, h):
-        return pltpu.make_async_copy(at(ww, 2, p, h), tails[2 * tail.index(p) + h], mvw_sem.at[p, h, 0])
+        kind, j = places.spot(p)
+        return pltpu.make_async_copy(at(ww, 2, p, h), tails[2 * kind + h].at[j], mvw_sem.at[p, h, 0])
 
     def update(p, h):
         for copy in moments(p, h):
@@ -272,7 +282,8 @@
     for p in spots:
         for i in range(2):
             onward_came(i, p).wait_recv()
-            across(4 + i, p).start()
+            if p < places.count - 1:
+                across(4 + i, p).start()
     for p in spots:
         for h in range(2):
             ahead(1 - h, p, h).wait_send()
@@ -284,7 +295,7 @@
             if p in tail:
                 hand(p, h).wait()
         for k in range(8):
-            if k in (0, 3) and p in tail:
+            if k in (0, 3) and p in tail or k in (4, 5) and p == places.count - 1:
                 continue
             across(k, p).wait_send()
             across_came(k, p).wait_recv()
@@ -298,7 +309,8 @@
     out = [jax.ShapeDtypeStruct(s, jnp.bfloat16) for s in shapes]
     out += [jax.ShapeDtypeStruct(one.shape, jnp.bfloat16) for one in m]
     out += [jax.ShapeDtypeStruct((8, 128), jnp.float32)]
-    out += [jax.ShapeDtypeStruct(places.piece[p // places.layers], jnp.bfloat16) for p in tail for _ in range(2)]
+    out += [jax.ShapeDtypeStruct((len(m), *k), jnp.bfloat16) for m, k in zip(places.members, places.kinds) for _ in range(2)]
+    out += [jax.ShapeDtypeStruct((2, *places.piece[-1]), jnp.bfloat16)]
     dma = pltpu.SemaphoreType.DMA
     half = jnp.bfloat16
     scratch = [
@@ -313,24 +325,197 @@
         functools.partial(exchange, places, tail, count),
         out_shape=out,
         in_specs=[anywhere] * 12,
-        out_specs=[anywhere] * 6 + [vmem] + [anywhere] * (2 * len(tail)),
+        out_specs=[anywhere] * 6 + [vmem] + [anywhere] * (2 * len(places.kinds) + 1),
         scratch_shapes=scratch,
         compiler_params=pltpu.CompilerParams(collective_id=0, has_side_effects=True, vmem_limit_bytes=66 * 1000 * 1000),
         name="exchange",
     )(*terms, *weights, *m, *v)
-    return got[:3], got[3:6], got[6], got[7:]
+    return got[:3], got[3:6], got[6], got[7:-1], got[-1]
+
+
+def params(**more):
+    return pltpu.CompilerParams(has_side_effects=False, **more)
+
+
+def finish(places, tail, *refs):
+    nk = len(places.kinds)
+    parts, i = [], 0
+    for size in (3, 3, 3, 3, 1, 3, 3, 3, nk, nk, nk, nk, 1, 1, 1, 1):
+        parts.append(refs[i : i + size])
+        i += size
+    whole, summed, m, v, (factor_ref,), out, new_m, new_v, slots, gg, mm, vv, (in_sem,), (out_sem,), (get_sem,), (put_sem,) = parts
+    n = places.n
+    chips = n // CORES
+    chip = lax.div(lax.axis_index(AXIS), CORES)
+    at = places.at
+
+    def gets(p, h):
+        refs = ((summed, gg), (m, mm), (v, vv))
+        return [pltpu.make_async_copy(places.own(a, p, h), at(b, 2, p, h), get_sem.at[p, h, j]) for j, (a, b) in enumerate(refs)]
+
+    def puts(p, h):
+        refs = ((mm, new_m), (vv, new_v))
+        return [pltpu.make_async_copy(at(a, 2, p, h), places.own(b, p, h), put_sem.at[p, h, j]) for j, (a, b) in enumerate(refs)]
+
+    pieces = [(p, h) for p in range(places.count) for h in range(2)]
+    items = []
+    for p, h in pieces:
+        for k in range(chips):
+            if p in tail and k == (1 if h else chips - 1) or p == places.count - 1 and k == 2:
+                continue
+            items += [(p, h, k, c) for c in range(CORES)]
+    used = [0] * nk
+    turn = []
+    for p, *_ in items:
+        kind = places.kinds.index(places.piece[p // places.layers])
+        turn.append((kind, used[kind]))
+        used[kind] += 1
+    of_kind = [[t for t, (k, _) in enumerate(turn) if k == kind] for kind in range(nk)]
+
+    def ends(t):
+        p, h, k, c = items[t]
+        block = lax.rem(chip + k, chips) * CORES + c
+        kind, u = turn[t]
+        return places.rows(whole, p, block, h), slots[kind].at[u % SLOTS], places.rows(out, p, block, h), (kind, u % SLOTS)
+
+    def read(t):
+        src, slot, _, sem = ends(t)
+        return pltpu.make_async_copy(src, slot, in_sem.at[sem])
+
+    def write(t):
+        _, slot, dst, sem = ends(t)
+        return pltpu.make_async_copy(slot, dst, out_sem.at[sem])
+
+    def start_read(t):
+        kind, u = turn[t]
+        if u >= SLOTS:
+            write(of_kind[kind][u - SLOTS]).wait()
+        read(t).start()
+
+    def update(p, h):
+        for copy in gets(p, h):
+            copy.wait()
+        gs, ms, vs = at(gg, 2, p, h), at(mm, 2, p, h), at(vv, 2, p, h)
+
+        def body(r, carry):
+            rows = pl.ds(pl.multiple_of(r * GROUP, GROUP), GROUP)
+            grad = gs[rows, :].astype(jnp.float32) * factor_ref[0:1, 0:1]
+            ms[rows, :] = 0.9 * ms[rows, :] + 0.1 * grad
+            vs[rows, :] = 0.95 * vs[rows, :] + 0.05 * grad * grad
+            return carry
+
+        lax.fori_loop(0, places.half[p // places.layers] // GROUP, body, 0)
+        for copy in puts(p, h):
+            copy.start()
+
+    for t in range(min(DEPTH, len(items))):
+        start_read(t)
+    for copy in gets(*pieces[0]):
+        copy.start()
+    done = 0
+    for t in range(len(items)):
+        read(t).wait()
+        write(t).start()
+        if t + DEPTH < len(items):
+            start_read(t + DEPTH)
+        while done < len(pieces) and (done + 1) * len(items) <= (t + 1) * len(pieces):
+            if done + 1 < len(pieces):
+                for copy in gets(*pieces[done + 1]):
+                    copy.start()
+            update(*pieces[done])
+            done += 1
+    for kind in range(nk):
+        for t in of_kind[kind][-SLOTS:]:
+            write(t).wait()
+    for p, h in pieces:
+        for copy in puts(p, h):
+            copy.wait()
+
+
+def finish_all(places, tail, whole, summed, m, v, factor):
+    anywhere, vmem = pl.BlockSpec(memory_space=pl.ANY), pl.BlockSpec(memory_space=pltpu.VMEM)
+    dma = pltpu.SemaphoreType.DMA
+    nk, f32 = len(places.kinds), jnp.float32
+    size = sum(w.size for w in whole)
+    mine = sum(one.size for one in m)
+    return pl.pallas_call(
+        functools.partial(finish, places, tail),
+        out_shape=[jax.ShapeDtypeStruct(w.shape, w.dtype) for w in whole] + [jax.ShapeDtypeStruct(one.shape, f32) for one in (*m, *v)],
+        in_specs=[anywhere] * 12 + [vmem],
+        out_specs=[anywhere] * 9,
+        scratch_shapes=[
+            *(pltpu.VMEM((SLOTS, *k), jnp.bfloat16) for k in places.kinds),
+            *places.scratch(2, jnp.bfloat16), *places.scratch(2, f32), *places.scratch(2, f32),
+            dma((nk, SLOTS)), dma((nk, SLOTS)), dma((places.count, 2, 3)), dma((places.count, 2, 2)),
+        ],
+        compiler_params=params(vmem_limit_bytes=58 * 1024 * 1024),
+        cost_estimate=pl.CostEstimate(flops=size * 100, bytes_accessed=size * 4 + mine * 18, transcendentals=0),
+        name="finish",
+    )(*whole, *summed, *m, *v, factor)
+
+
+def place_late(places, spots, *refs):
+    k = len(spots)
+    arrays, out, sem = refs[:k], refs[k + 3 : k + 6], refs[k + 6]
+    chips = places.n // CORES
+    me = lax.axis_index(AXIS)
+    core, chip = lax.rem(me, CORES), lax.div(me, CORES)
+    copies = []
+    for array, pieces in zip(arrays, spots):
+        for j, (p, h, away, other) in enumerate(pieces):
+            block = lax.rem(chip + (away + chips), chips) * CORES + (1 - core if other else core)
+            copies.append(pltpu.make_async_copy(array.at[j], places.rows(out, p, block, h), sem.at[len(copies)]))
+    for copy in copies:
+        copy.start()
+    for copy in copies:
+        copy.wait()
+
+
+def place_all(places, spots, arrays, out):
+    anywhere, vmem = pl.BlockSpec(memory_space=pl.ANY), pl.BlockSpec(memory_space=pltpu.VMEM)
+    k = len(spots)
+    return pl.pallas_call(
+        functools.partial(place_late, places, spots),
+        out_shape=[jax.ShapeDtypeStruct(w.shape, w.dtype) for w in out],
+        in_specs=[vmem] * k + [anywhere] * 3,
+        out_specs=[anywhere] * 3,
+        input_output_aliases={k + j: j for j in range(3)},
+        scratch_shapes=[pltpu.SemaphoreType.DMA((sum(len(one) for one in spots),))],
+        compiler_params=params(vmem_limit_bytes=16 * 1024 * 1024),
+        cost_estimate=pl.CostEstimate(flops=10**7, bytes_accessed=sum(x.size for x in arrays) * 4, transcendentals=0),
+        name="place_late",
+    )(*arrays, *out)
 
 
 def solution(mesh):
     n = mesh.shape[AXIS]
+    chips = n // CORES
 
     def step(*arrays):
         terms, weights, m, v = (arrays[i : i + 3] for i in (0, 3, 6, 9))
-        whole, summed, factor, _ = gather_new([t[0] for t in terms], weights, m, v, n, [])
-        grads = [g.astype(jnp.float32) * factor[0, 0] for g in summed]
-        new_m = [0.9 * a + 0.1 * g for a, g in zip(m, grads)]
-        new_v = [0.95 * a + 0.05 * g * g for a, g in zip(v, grads)]
-        return (*whole, *new_m, *new_v)
+        places = Places(n, [w.shape for w in weights])
+        tail = list(range(places.count))
+        whole, summed, factor, late, last = gather_new([t[0] for t in terms], weights, m, v, n, tail)
+        kinds = range(len(places.kinds))
+        shift = [[(j, (j // CORES + s) % chips * CORES + j % CORES) for j in range(n)] for s in (1, -1)]
+        swap = [(j, j // CORES * CORES + (CORES - 1 - j % CORES)) for j in range(n)]
+        came = []
+        for k in kinds:
+            came.append([lax.ppermute(late[2 * k + h], AXIS, shift[h]) for h in range(2)])
+        last_swapped = lax.ppermute(last, AXIS, swap)
+        *out, m0, m1, m2, v0, v1, v2 = finish_all(places, tail, whole, summed, m, v, factor)
+        end = places.count - 1
+        spots = lambda k, other: [[(p, h, -1 if h == 0 else 1, other) for p in places.members[k]] for h in range(2)]
+        ends = lambda other: [(end, 1 - i, 2, other) for i in range(2)]
+        for k in kinds:
+            here, out = lax.optimization_barrier((came[k], out))
+            swapped = [lax.ppermute(piece, AXIS, swap) for piece in here]
+            if k == 0:
+                out = place_all(places, [*spots(k, False), ends(False), ends(True)], [*here, last, last_swapped], out)
+            else:
+                out = place_all(places, spots(k, False), here, out)
+            out = place_all(places, spots(k, True), swapped, out)
+        return (*out, m0, m1, m2, v0, v1, v2)
 
     all_of, cut = P(None, None, None), P(None, AXIS, None)
     return jax.shard_map(

time: 339 us -> 313 us (0.923)
  local copies, waits for them, and re-layouts: 20.9 us -> 0.01 us
  other arithmetic: 18.5 us -> 0 us
  waiting for transfers between devices: 0 us -> 14 us
  Pallas kernels: 299 us -> 290 us
  starting transfers between devices: 0 us -> 8.5 us
    pallas_call x1, Pallas kernels: 299 us -> 250 us  [gather_new(): pl.pallas_call(functools.partial(exchange, places, tail, count), out_shap...]
    pallas_call x0 -> x5, Pallas kernels: none -> 39.7 us  [the longest x1 33.7 us: finish_all(): pl.pallas_call(functools.partial(finish, places, tail), out_shape=[jax.Sh...]
    unnamed x21 -> x6, local copies, waits for them, and re-layouts: 19.8 us -> 0.01 us
    add x2 -> x0, other arithmetic: 18.5 us -> none  [step(): new_v = [0.95 * a + 0.05 * g * g for a, g in zip(v, grads)]]
    ppermute x0 -> x9, waiting for transfers between devices: none -> 14 us  [the longest x4 9.55 us: step(): lax.ppermute(late[2 * k + h], AXIS, shift[h])]
    ppermute x0 -> x9, starting transfers between devices: none -> 8.5 us  [the longest x4 5.43 us: step(): lax.ppermute(late[2 * k + h], AXIS, shift[h])]
  transfers between devices with their start and end apart: 0 -> 9, of which waited for: 0 -> 4; matrix products, arithmetic and copies ran while one was open for 0% -> 0% of each run, Pallas kernels for 0% -> 12%
where the time goes in v2:
time: 313 us
  Pallas kernels  290 us (93%)
  waiting for transfers between devices  14 us (4%)
  starting transfers between devices  8.5 us (3%)
    pallas_call x1, Pallas kernels, gather_new(): pl.pallas_call(functools.partial(exchange, places, tail, count), out_shap...  250 us
    pallas_call x1, Pallas kernels, finish_all(): pl.pallas_call(functools.partial(finish, places, tail), out_shape=[jax.Sh...  33.7 us
    ppermute x4, waiting for transfers between devices, step(): lax.ppermute(late[2 * k + h], AXIS, shift[h])  9.55 us
  transfers between devices with their start and end apart: 9, of which 4 were waited for; matrix products, arithmetic and copies ran while one was open for 0% of the time, Pallas kernels for 12%

profile of v2, /device:TPU:113, one launch (start us, length us, event | category | flops | bytes accessed | tf_op | source)
XLA Modules:
  0.0 313.0 jit_solution(9511147292043323332)
XLA Ops:
  0.6 250.0 %exchange.1 = (bf16[2,1024,2816]{2,1,0:T(8,128)(2,1)}, bf16[2,1024,2816]{2,1,0:T(8,128)(2,1)}, bf16[2,2816,1024]{2,1,0:T(8,128)(2,1)}, bf16[2,128,2816]{2,1,0:T(...) custom-call(bf16[2,1024,2816]{2,1,0:T(8,128)(2,1)} %bitcast.3, ...), custom_call_target="tpu_custom_call" | custom-call | tf_op jit(solution)/shard_map/exchange/pallas_call | solution.py:324
  250.7 0.4 collective-permute-start.2
  251.1 2.3 collective-permute-start.3
  253.5 0.0 copy-start
  253.5 0.0 copy-start.2
  253.5 0.0 copy-start.1
  253.5 33.7 %finish.1 = (bf16[2,1024,2816]{2,1,0:T(8,128)(2,1)}, bf16[2,1024,2816]{2,1,0:T(8,128)(2,1)}, bf16[2,2816,1024]{2,1,0:T(8,128)(2,1)}, f32[2,128,2816]{2,1,0:T(8,1...) custom-call(bf16[2,1024,2816]{2,1,0:T(8,128)(2,1)} %get-tuple-elemen, ...), custom_call_target="tpu_custom_call" | custom-call | flops 1730150400 | bytes 108134400 | tf_op jit(solution)/shard_map/finish/pallas_call | solution.py:441
  287.1 0.0 collective-permute-done.2.refs_0_
  287.2 0.0 collective-permute-done.3.refs_1_
  287.2 1.6 collective-permute-start.4
  288.8 0.1 collective-permute-start.5
  288.9 0.0 copy-done
  288.9 0.4 collective-permute-start.6
  289.3 0.0 copy-done.2
  289.3 0.0 collective-permute-start
  289.3 0.0 copy-done.1
  289.3 2.7 collective-permute-start.1
  292.0 2.7 collective-permute-done.6.refs_3_
  294.7 2.1 place_late.4
  296.9 0.0 collective-permute-done.4.refs_0_
  296.9 0.0 collective-permute-done.5.refs_1_
  296.9 1.7 place_late.5
  298.6 9.5 %collective-permute-done.refs_0_ = bf16[2,176,1024]{2,1,0:T(8,128)(2,1)S(1)} collective-permute-done((bf16[2,176,1024]{2,1,0:T(8,128)(2,1)S(1)}, bf16[2,176,1024]{2,1,0:T(8,128)(2,1)S(1)}, u32[]{:S(2)}, u32[]{:S(2)}) %collective-permute-start) | collective-permute-done | bytes 720928 | tf_op jit(solution)/shard_map/ppermute | solution.py:504
  308.1 0.0 collective-permute-done.1.refs_1_
  308.1 1.0 collective-permute-start.7
  309.1 0.0 collective-permute-start.8
  309.1 1.1 place_late.6
  310.2 0.7 collective-permute-done.7.refs_0_
  310.9 1.0 collective-permute-done.8.refs_1_
  311.9 1.1 place_late.7
Async XLA Ops:
  250.7 36.5 %collective-permute-start.2 = (bf16[4,64,2816]{2,1,0:T(8,128)(2,1)}, bf16[4,64,2816]{2,1,0:T(8,128)(2,1)S(1)}, u32[]{:S(2)}, u32[]{:S(2)}) collective-permute-start(bf16[4,64,2816]{2,1,0:T(8,128)(2,1)} %get-tuple-element.54), channel_id=1, source_target_pairs={{0,2},{1,3},{2,4},{3,5},{4,6},{5,7},{6,0},{7,1},{8,10},{9,11},{10,... | collective-permute-start | bytes 4325384 | tf_op jit(solution)/shard_map/ppermute | solution.py:504
  251.1 36.0 %collective-permute-start.3 = (bf16[4,64,2816]{2,1,0:T(8,128)(2,1)}, bf16[4,64,2816]{2,1,0:T(8,128)(2,1)S(1)}, u32[]{:S(2)}, u32[]{:S(2)}) collective-permute-start(bf16[4,64,2816]{2,1,0:T(8,128)(2,1)} %get-tuple-element.55), channel_id=1, source_target_pairs={{0,6},{1,7},{2,0},{3,1},{4,2},{5,3},{6,4},{7,5},{8,14},{9,15},{10,... | collective-permute-start | bytes 4325384 | tf_op jit(solution)/shard_map/ppermute | solution.py:504
  253.5 35.4 %copy-start = (bf16[2,176,1024]{2,1,0:T(8,128)(2,1)S(1)}, bf16[2,176,1024]{2,1,0:T(8,128)(2,1)}, u32[]{:S(2)}) copy-start(bf16[2,176,1024]{2,1,0:T(8,128)(2,1)} %get-tuple-element.68.refs_2_) | copy-start | bytes 2162692
  253.5 35.8 %copy-start.2 = (bf16[2,176,1024]{2,1,0:T(8,128)(2,1)S(1)}, bf16[2,176,1024]{2,1,0:T(8,128)(2,1)}, u32[]{:S(2)}) copy-start(bf16[2,176,1024]{2,1,0:T(8,128)(2,1)} %get-tuple-element.52) | copy-start | bytes 2162692
  253.5 35.8 %copy-start.1 = (bf16[2,176,1024]{2,1,0:T(8,128)(2,1)S(1)}, bf16[2,176,1024]{2,1,0:T(8,128)(2,1)}, u32[]{:S(2)}) copy-start(bf16[2,176,1024]{2,1,0:T(8,128)(2,1)} %get-tuple-element.53) | copy-start | bytes 2162692
  287.2 9.7 %collective-permute-start.4 = (bf16[4,64,2816]{2,1,0:T(8,128)(2,1)S(1)}, bf16[4,64,2816]{2,1,0:T(8,128)(2,1)S(1)}, u32[]{:S(2)}, u32[]{:S(2)}) collective-permute-start(bf16[4,64,2816]{2,1,0:T(8,128)(2,1)S(1)} %collective-permute-done.2.refs_0_), channel_id=1, source_target_pairs={{0,1},{1,0},{2,3},{3,2},{4,5},{5,4},{6,7},{7,6},{8,9},{9,8},{10,11... | collective-permute-start | bytes 4325384 | tf_op jit(solution)/shard_map/ppermute | solution.py:512
  288.8 8.1 %collective-permute-start.5 = (bf16[4,64,2816]{2,1,0:T(8,128)(2,1)S(1)}, bf16[4,64,2816]{2,1,0:T(8,128)(2,1)S(1)}, u32[]{:S(2)}, u32[]{:S(2)}) collective-permute-start(bf16[4,64,2816]{2,1,0:T(8,128)(2,1)S(1)} %collective-permute-done.3.refs_1_), channel_id=1, source_target_pairs={{0,1},{1,0},{2,3},{3,2},{4,5},{5,4},{6,7},{7,6},{8,9},{9,8},{10,11... | collective-permute-start | bytes 4325384 | tf_op jit(solution)/shard_map/ppermute | solution.py:512
  288.9 5.8 %collective-permute-start.6 = (bf16[2,176,1024]{2,1,0:T(8,128)(2,1)S(1)}, bf16[2,176,1024]{2,1,0:T(8,128)(2,1)S(1)}, u32[]{:S(2)}, u32[]{:S(2)}) collective-permute-start(bf16[2,176,1024]{2,1,0:T(8,128)(2,1)S(1)} %copy-done), channel_id=1, source_target_pairs={{0,1},{1,0},{2,3},{3,2},{4,5},{5,4},{6,7},{7,6},{8,9},{9,8},{10,11... | collective-permute-start | bytes 2162696 | tf_op jit(solution)/shard_map/ppermute | solution.py:505
  289.3 18.8 %collective-permute-start = (bf16[2,176,1024]{2,1,0:T(8,128)(2,1)S(1)}, bf16[2,176,1024]{2,1,0:T(8,128)(2,1)S(1)}, u32[]{:S(2)}, u32[]{:S(2)}) collective-permute-start(bf16[2,176,1024]{2,1,0:T(8,128)(2,1)S(1)} %copy-done.2), channel_id=1, source_target_pairs={{0,2},{1,3},{2,4},{3,5},{4,6},{5,7},{6,0},{7,1},{8,10},{9,11},{10,... | collective-permute-start | bytes 2162696 | tf_op jit(solution)/shard_map/ppermute | solution.py:504
  289.3 18.8 %collective-permute-start.1 = (bf16[2,176,1024]{2,1,0:T(8,128)(2,1)S(1)}, bf16[2,176,1024]{2,1,0:T(8,128)(2,1)S(1)}, u32[]{:S(2)}, u32[]{:S(2)}) collective-permute-start(bf16[2,176,1024]{2,1,0:T(8,128)(2,1)S(1)} %copy-done.1), channel_id=1, source_target_pairs={{0,6},{1,7},{2,0},{3,1},{4,2},{5,3},{6,4},{7,5},{8,14},{9,15},{10,... | collective-permute-start | bytes 2162696 | tf_op jit(solution)/shard_map/ppermute | solution.py:504
  308.1 2.8 collective-permute-start.7
  309.1 2.8 collective-permute-start.8

commit v3 on v2

--- a/solution.py
+++ b/solution.py
@@ -34,6 +34,8 @@
         self.kinds = sorted(set(self.piece), key=self.piece.index)
         self.members = [[p for p in range(self.count) if self.piece[p // self.layers] == k] for k in self.kinds]
 
+        self.end = self.count - 1
+
     def scratch(self, slots, dtype):
         return [pltpu.VMEM((len(m) * slots, *k), dtype) for m, k in zip(self.members, self.kinds)]
 
@@ -57,14 +59,14 @@
 
 def exchange(places, tail, count, *refs):
     nk = len(places.kinds)
-    names = (3, 3, 3, 3, 3, 3, 1, 2 * nk + 1, nk, nk, nk, nk, nk, nk, nk, 1, 1, 1, 1, 1, 1, 1, 1, 1)
+    names = (3, 3, 3, 3, 3, nk, nk, 1, 2 * nk + 1, nk, nk, nk, nk, nk, 1, 1, 1, 1, 1, 1, 1, 1, 1)
     parts, i = [], 0
     for size in names:
         parts.append(refs[i : i + size])
         i += size
-    g, w, m, v, whole, summed, (factor_ref,), (*tails, last) = parts[:8]
-    own, par, got, mm, vv, ww, acc = parts[8:15]
-    (sq,), (own_sem,), (par_send,), (par_recv,), (snd,), (rcv,), (mvw_sem,), (sq_send,), (sq_recv,) = parts[15:]
+    g, w, m, v, whole, mm, vv, (factor_ref,), (*tails, last) = parts[:9]
+    own, par, got, ww, acc = parts[9:14]
+    (sq,), (own_sem,), (par_send,), (par_recv,), (snd,), (rcv,), (mvw_sem,), (sq_send,), (sq_recv,) = parts[14:]
 
     n, at = places.n, places.at
     chips = n // CORES
@@ -208,12 +210,16 @@
 
     def onward(i, p):
         here = places.rows(whole, p, away(-sign[i], core), 1 - i)
-        there = last.at[i] if p == places.count - 1 else here
+        there = last.at[i] if p == places.end else here
         return remote(here, there, snd.at[p, 4 + i], rcv.at[p, 4 + i], beside[i])
 
     def onward_came(i, p):
-        here = last.at[i] if p == places.count - 1 else places.rows(whole, p, away(2, core), 1 - i)
+        here = last.at[i] if p == places.end else places.rows(whole, p, away(2, core), 1 - i)
         return remote(here, here, snd.at[p, 4 + i], rcv.at[p, 4 + i], beside[i])
+
+    def extra(i):
+        here = places.rows(whole, places.end, away(-sign[i], 1 - core), 1 - i)
+        return remote(here, last.at[2 + i], snd.at[places.end, 3 * i], rcv.at[places.end, 3 * i], beside[i])
 
     def across(k, p):
         if k < 4:
@@ -235,10 +241,7 @@
         return remote(here, here, par_send.at[p, k], par_recv.at[p, k], partner)
 
     def keep(p, h):
-        return [
-            pltpu.make_async_copy(at(ww, 2, p, h), places.rows(whole, p, me, h), own_sem.at[p, h]),
-            pltpu.make_async_copy(at(own, 4, p, 3 - h), places.own(summed, p, h), own_sem.at[p, 2 + h]),
-        ]
+        return [pltpu.make_async_copy(at(ww, 2, p, h), places.rows(whole, p, me, h), own_sem.at[p, h])]
 
     def hand(p, h):
         kind, j = places.spot(p)
@@ -252,7 +255,7 @@
         def body(r, carry):
             rows = pl.ds(pl.multiple_of(r * GROUP, GROUP), GROUP)
             grad = gs[rows, :].astype(jnp.float32) * factor_ref[0:1, 0:1]
-            ws[rows, :] = adamw(ws[rows, :].astype(jnp.float32), ms[rows, :], vs[rows, :], grad)[0]
+            ws[rows, :], ms[rows, :], vs[rows, :] = adamw(ws[rows, :].astype(jnp.float32), ms[rows, :], vs[rows, :], grad)
             return carry
 
         lax.fori_loop(0, places.half[p // places.layers] // GROUP, body, 0)
@@ -270,35 +273,61 @@
     for p in later:
         for h in (0, 1):
             ahead(h, p, h).start()
-    for p in spots:
+    end, second = places.end, core == CORES - 1
+    for p in spots[:-1]:
         for i in range(2):
             ahead_came(i, p, 1 - i).wait_recv()
             onward(i, p).start()
             across(2 * i + 1 - i, p).start()
+    for i in range(2):
+        ahead_came(i, end, 1 - i).wait_recv()
+        across(2 * i + 1 - i, end).start()
+
+    @pl.when(second)
+    def _():
+        for i in range(2):
+            onward(i, end).start()
+        for i in range(2):
+            across_came(2 * i + 1 - i, end).wait_recv()
+            extra(i).start()
+
     for p in later:
         for i in range(2):
             ahead_came(i, p, i).wait_recv()
             across(2 * i + i, p).start()
-    for p in spots:
+    for p in spots[:-1]:
         for i in range(2):
             onward_came(i, p).wait_recv()
-            if p < places.count - 1:
-                across(4 + i, p).start()
+            across(4 + i, p).start()
+
+    @pl.when(second)
+    def _():
+        for i in range(2):
+            for copy in (onward(i, end), extra(i)):
+                copy.wait()
+
+    @pl.when(jnp.logical_not(second))
+    def _():
+        for i in range(2):
+            across_came(2 * i + 1 - i, end).wait_recv()
+
     for p in spots:
         for h in range(2):
             ahead(1 - h, p, h).wait_send()
             if p in later:
                 ahead(h, p, h).wait_send()
-            onward(h, p).wait_send()
+            if p != end:
+                onward(h, p).wait_send()
             for copy in keep(p, h):
                 copy.wait()
             if p in tail:
                 hand(p, h).wait()
         for k in range(8):
-            if k in (0, 3) and p in tail or k in (4, 5) and p == places.count - 1:
+            if k in (0, 3) and p in tail or k in (4, 5) and p == places.end:
                 continue
             across(k, p).wait_send()
-            across_came(k, p).wait_recv()
+            if k not in (1, 2) or p != end:
+                across_came(k, p).wait_recv()
 
 
 def gather_new(terms, weights, m, v, n, tail):
@@ -306,16 +335,16 @@
     places = Places(n, shapes)
     count = float(sum(w.size for w in weights))
     anywhere, vmem = pl.BlockSpec(memory_space=pl.ANY), pl.BlockSpec(memory_space=pltpu.VMEM)
-    out = [jax.ShapeDtypeStruct(s, jnp.bfloat16) for s in shapes]
-    out += [jax.ShapeDtypeStruct(one.shape, jnp.bfloat16) for one in m]
+    out = [pltpu.HBM(s, jnp.bfloat16) for s in shapes]
+    out += places.scratch(2, jnp.float32) * 2
     out += [jax.ShapeDtypeStruct((8, 128), jnp.float32)]
     out += [jax.ShapeDtypeStruct((len(m), *k), jnp.bfloat16) for m, k in zip(places.members, places.kinds) for _ in range(2)]
-    out += [jax.ShapeDtypeStruct((2, *places.piece[-1]), jnp.bfloat16)]
+    out += [jax.ShapeDtypeStruct((4, *places.piece[-1]), jnp.bfloat16)]
     dma = pltpu.SemaphoreType.DMA
-    half = jnp.bfloat16
+    half, nk = jnp.bfloat16, len(places.kinds)
     scratch = [
         *places.scratch(4, half), *places.scratch(8, half), *places.scratch(6, half),
-        *places.scratch(2, jnp.float32), *places.scratch(2, jnp.float32), *places.scratch(2, half),
+        *places.scratch(2, half),
         *(pltpu.VMEM((GROUP, k[1]), jnp.float32) for k in places.kinds),
         pltpu.VMEM((n, 8, 128), jnp.float32),
         dma((places.count, 4)), dma((places.count, 8)), dma((places.count, 8)), dma((places.count, 6)), dma((places.count, 6)),
@@ -325,12 +354,13 @@
         functools.partial(exchange, places, tail, count),
         out_shape=out,
         in_specs=[anywhere] * 12,
-        out_specs=[anywhere] * 6 + [vmem] + [anywhere] * (2 * len(places.kinds) + 1),
+        out_specs=[anywhere] * 3 + [vmem] * (2 * nk + 1) + [anywhere] * (2 * nk + 1),
         scratch_shapes=scratch,
-        compiler_params=pltpu.CompilerParams(collective_id=0, has_side_effects=True, vmem_limit_bytes=66 * 1000 * 1000),
+        compiler_params=pltpu.CompilerParams(collective_id=0, has_side_effects=True, vmem_limit_bytes=46 * 1000 * 1000),
         name="exchange",
     )(*terms, *weights, *m, *v)
-    return got[:3], got[3:6], got[6], got[7:-1], got[-1]
+    got_m, got_v, rest = got[3 : 3 + nk], got[3 + nk : 3 + 2 * nk], got[4 + 2 * nk :]
+    return got[:3], got_m, got_v, rest[:-1], rest[-1]
 
 
 def params(**more):
@@ -340,37 +370,30 @@
 def finish(places, tail, *refs):
     nk = len(places.kinds)
     parts, i = [], 0
-    for size in (3, 3, 3, 3, 1, 3, 3, 3, nk, nk, nk, nk, 1, 1, 1, 1):
+    for size in (3, nk, nk, 3, 3, 3, nk, 1, 1, 1):
         parts.append(refs[i : i + size])
         i += size
-    whole, summed, m, v, (factor_ref,), out, new_m, new_v, slots, gg, mm, vv, (in_sem,), (out_sem,), (get_sem,), (put_sem,) = parts
+    whole, mm, vv, out, new_m, new_v, slots, (in_sem,), (out_sem,), (put_sem,) = parts
     n = places.n
     chips = n // CORES
     chip = lax.div(lax.axis_index(AXIS), CORES)
-    at = places.at
-
-    def gets(p, h):
-        refs = ((summed, gg), (m, mm), (v, vv))
-        return [pltpu.make_async_copy(places.own(a, p, h), at(b, 2, p, h), get_sem.at[p, h, j]) for j, (a, b) in enumerate(refs)]
+    pieces = [(p, h) for p in range(places.count) for h in range(2)]
 
     def puts(p, h):
         refs = ((mm, new_m), (vv, new_v))
-        return [pltpu.make_async_copy(at(a, 2, p, h), places.own(b, p, h), put_sem.at[p, h, j]) for j, (a, b) in enumerate(refs)]
-
-    pieces = [(p, h) for p in range(places.count) for h in range(2)]
+        return [pltpu.make_async_copy(places.at(a, 2, p, h), places.own(b, p, h), put_sem.at[p, h, j]) for j, (a, b) in enumerate(refs)]
+
     items = []
     for p, h in pieces:
         for k in range(chips):
-            if p in tail and k == (1 if h else chips - 1) or p == places.count - 1 and k == 2:
+            if p in tail and k == (1 if h else chips - 1) or p == places.end and k == 2:
                 continue
             items += [(p, h, k, c) for c in range(CORES)]
-    used = [0] * nk
-    turn = []
-    for p, *_ in items:
-        kind = places.kinds.index(places.piece[p // places.layers])
-        turn.append((kind, used[kind]))
-        used[kind] += 1
-    of_kind = [[t for t, (k, _) in enumerate(turn) if k == kind] for kind in range(nk)]
+    turn, of_kind = [], [[] for _ in range(nk)]
+    for t, (p, *_) in enumerate(items):
+        kind, _ = places.spot(p)
+        turn.append((kind, len(of_kind[kind])))
+        of_kind[kind].append(t)
 
     def ends(t):
         p, h, k, c = items[t]
@@ -392,37 +415,17 @@
             write(of_kind[kind][u - SLOTS]).wait()
         read(t).start()
 
-    def update(p, h):
-        for copy in gets(p, h):
-            copy.wait()
-        gs, ms, vs = at(gg, 2, p, h), at(mm, 2, p, h), at(vv, 2, p, h)
-
-        def body(r, carry):
-            rows = pl.ds(pl.multiple_of(r * GROUP, GROUP), GROUP)
-            grad = gs[rows, :].astype(jnp.float32) * factor_ref[0:1, 0:1]
-            ms[rows, :] = 0.9 * ms[rows, :] + 0.1 * grad
-            vs[rows, :] = 0.95 * vs[rows, :] + 0.05 * grad * grad
-            return carry
-
-        lax.fori_loop(0, places.half[p // places.layers] // GROUP, body, 0)
-        for copy in puts(p, h):
-            copy.start()
-
     for t in range(min(DEPTH, len(items))):
         start_read(t)
-    for copy in gets(*pieces[0]):
-        copy.start()
     done = 0
     for t in range(len(items)):
         read(t).wait()
         write(t).start()
         if t + DEPTH < len(items):
             start_read(t + DEPTH)
-        while done < len(pieces) and (done + 1) * len(items) <= (t + 1) * len(pieces):
-            if done + 1 < len(pieces):
-                for copy in gets(*pieces[done + 1]):
-                    copy.start()
-            update(*pieces[done])
+        while done * len(items) < (t + 1) * len(pieces) and done < len(pieces):
+            for copy in puts(*pieces[done]):
+                copy.start()
             done += 1
     for kind in range(nk):
         for t in of_kind[kind][-SLOTS:]:
@@ -432,26 +435,27 @@
             copy.wait()
 
 
-def finish_all(places, tail, whole, summed, m, v, factor):
+def finish_all(places, tail, whole, mm, vv, m, v):
     anywhere, vmem = pl.BlockSpec(memory_space=pl.ANY), pl.BlockSpec(memory_space=pltpu.VMEM)
     dma = pltpu.SemaphoreType.DMA
-    nk, f32 = len(places.kinds), jnp.float32
+    nk = len(places.kinds)
     size = sum(w.size for w in whole)
     mine = sum(one.size for one in m)
+    whole = [pltpu.with_memory_space_constraint(w, pltpu.HBM) for w in whole]
+    mm, vv = ([pltpu.with_memory_space_constraint(one, pltpu.VMEM) for one in x] for x in (mm, vv))
     return pl.pallas_call(
         functools.partial(finish, places, tail),
-        out_shape=[jax.ShapeDtypeStruct(w.shape, w.dtype) for w in whole] + [jax.ShapeDtypeStruct(one.shape, f32) for one in (*m, *v)],
-        in_specs=[anywhere] * 12 + [vmem],
+        out_shape=[jax.ShapeDtypeStruct(a.shape, a.dtype) for a in (*whole, *m, *v)],
+        in_specs=[anywhere] * 3 + [vmem] * (2 * nk),
         out_specs=[anywhere] * 9,
         scratch_shapes=[
             *(pltpu.VMEM((SLOTS, *k), jnp.bfloat16) for k in places.kinds),
-            *places.scratch(2, jnp.bfloat16), *places.scratch(2, f32), *places.scratch(2, f32),
-            dma((nk, SLOTS)), dma((nk, SLOTS)), dma((places.count, 2, 3)), dma((places.count, 2, 2)),
+            dma((nk, SLOTS)), dma((nk, SLOTS)), dma((places.count, 2, 2)),
         ],
-        compiler_params=params(vmem_limit_bytes=58 * 1024 * 1024),
-        cost_estimate=pl.CostEstimate(flops=size * 100, bytes_accessed=size * 4 + mine * 18, transcendentals=0),
+        compiler_params=params(vmem_limit_bytes=24 * 1024 * 1024),
+        cost_estimate=pl.CostEstimate(flops=size * 100, bytes_accessed=size * 4 + mine * 8, transcendentals=0),
         name="finish",
-    )(*whole, *summed, *m, *v, factor)
+    )(*whole, *mm, *vv)
 
 
 def place_late(places, spots, *refs):
@@ -460,15 +464,22 @@
     chips = places.n // CORES
     me = lax.axis_index(AXIS)
     core, chip = lax.rem(me, CORES), lax.div(me, CORES)
-    copies = []
-    for array, pieces in zip(arrays, spots):
-        for j, (p, h, away, other) in enumerate(pieces):
-            block = lax.rem(chip + (away + chips), chips) * CORES + (1 - core if other else core)
-            copies.append(pltpu.make_async_copy(array.at[j], places.rows(out, p, block, h), sem.at[len(copies)]))
-    for copy in copies:
-        copy.start()
-    for copy in copies:
-        copy.wait()
+    jobs = {}
+    for array, (only, pieces) in zip(arrays, spots):
+        for j, (p, h, away, which) in enumerate(pieces):
+            block = lax.rem(chip + (away + chips), chips) * CORES + (lax.rem(core + which[1], CORES) if which[0] else which[1])
+            mine = jobs.setdefault(only, [])
+            mine.append(pltpu.make_async_copy(array.at[j], places.rows(out, p, block, h), sem.at[sum(len(x) for x in jobs.values())]))
+
+    for only, copies in jobs.items():
+
+        def run():
+            for copy in copies:
+                copy.start()
+            for copy in copies:
+                copy.wait()
+
+        run() if only is None else pl.when(core == only)(run)
 
 
 def place_all(places, spots, arrays, out):
@@ -480,7 +491,7 @@
         in_specs=[vmem] * k + [anywhere] * 3,
         out_specs=[anywhere] * 3,
         input_output_aliases={k + j: j for j in range(3)},
-        scratch_shapes=[pltpu.SemaphoreType.DMA((sum(len(one) for one in spots),))],
+        scratch_shapes=[pltpu.SemaphoreType.DMA((sum(len(one) for _, one in spots),))],
         compiler_params=params(vmem_limit_bytes=16 * 1024 * 1024),
         cost_estimate=pl.CostEstimate(flops=10**7, bytes_accessed=sum(x.size for x in arrays) * 4, transcendentals=0),
         name="place_late",
@@ -495,7 +506,7 @@
         terms, weights, m, v = (arrays[i : i + 3] for i in (0, 3, 6, 9))
         places = Places(n, [w.shape for w in weights])
         tail = list(range(places.count))
-        whole, summed, factor, late, last = gather_new([t[0] for t in terms], weights, m, v, n, tail)
+        whole, mm, vv, late, last = gather_new([t[0] for t in terms], weights, m, v, n, tail)
         kinds = range(len(places.kinds))
         shift = [[(j, (j // CORES + s) % chips * CORES + j % CORES) for j in range(n)] for s in (1, -1)]
         swap = [(j, j // CORES * CORES + (CORES - 1 - j % CORES)) for j in range(n)]
@@ -503,18 +514,18 @@
         for k in kinds:
             came.append([lax.ppermute(late[2 * k + h], AXIS, shift[h]) for h in range(2)])
         last_swapped = lax.ppermute(last, AXIS, swap)
-        *out, m0, m1, m2, v0, v1, v2 = finish_all(places, tail, whole, summed, m, v, factor)
-        end = places.count - 1
-        spots = lambda k, other: [[(p, h, -1 if h == 0 else 1, other) for p in places.members[k]] for h in range(2)]
-        ends = lambda other: [(end, 1 - i, 2, other) for i in range(2)]
+        *out, m0, m1, m2, v0, v1, v2 = finish_all(places, tail, whole, mm, vv, m, v)
+        own, other = (True, 0), (True, 1)
+        spots = lambda k, which: [(None, [(p, h, -1 if h == 0 else 1, which) for p in places.members[k]]) for h in range(2)]
+        ends = [(places.end, 1 - i, 2, (False, c)) for c in (1, 0) for i in range(2)]
         for k in kinds:
             here, out = lax.optimization_barrier((came[k], out))
             swapped = [lax.ppermute(piece, AXIS, swap) for piece in here]
             if k == 0:
-                out = place_all(places, [*spots(k, False), ends(False), ends(True)], [*here, last, last_swapped], out)
+                out = place_all(places, [*spots(k, own), (1, ends), (0, ends)], [*here, last, last_swapped], out)
             else:
-                out = place_all(places, spots(k, False), here, out)
-            out = place_all(places, spots(k, True), swapped, out)
+                out = place_all(places, spots(k, own), here, out)
+            out = place_all(places, spots(k, other), swapped, out)
         return (*out, m0, m1, m2, v0, v1, v2)
 
     all_of, cut = P(None, None, None), P(None, AXIS, None)

time: 313 us -> 306 us (0.978)
  Pallas kernels: 290 us -> 281 us
  waiting for transfers between devices: 14 us -> 17.4 us
    pallas_call x1, Pallas kernels: 33.7 us -> 24 us  [finish_all(): pl.pallas_call(functools.partial(finish, places, tail), out_shape=[jax.Sh...]
    ppermute x4, waiting for transfers between devices: 9.55 us -> 15.7 us  [step(): lax.ppermute(late[2 * k + h], AXIS, shift[h])]
  transfers between devices with their start and end apart: 9 -> 9, of which waited for: 4 -> 4; matrix products, arithmetic and copies ran while one was open for 0% -> 0% of each run, Pallas kernels for 12% -> 10%
where the time goes in v3:
time: 306 us
  Pallas kernels  281 us (92%)
  waiting for transfers between devices  17.4 us (6%)
  starting transfers between devices  6.89 us (2%)
    pallas_call x1, Pallas kernels, gather_new(): pl.pallas_call(functools.partial(exchange, places, tail, count), out_shap...  250 us
    pallas_call x1, Pallas kernels, finish_all(): pl.pallas_call(functools.partial(finish, places, tail), out_shape=[jax.Sh...  24 us
    ppermute x4, waiting for transfers between devices, step(): lax.ppermute(late[2 * k + h], AXIS, shift[h])  15.7 us
    pallas_call x4, Pallas kernels, place_all(): pl.pallas_call(functools.partial(place_late, places, spots), out_shape=[j...  6.7 us
  transfers between devices with their start and end apart: 9, of which 4 were waited for; matrix products, arithmetic and copies ran while one was open for 0% of the time, Pallas kernels for 10%

profile of v3, /device:TPU:113, one launch (start us, length us, event | category | flops | bytes accessed | tf_op | source)
XLA Modules:
  0.0 306.1 jit_solution(3984734348365841415)
XLA Ops:
  0.6 250.4 %exchange.1 = (bf16[2,1024,2816]{2,1,0:T(8,128)(2,1)}, bf16[2,1024,2816]{2,1,0:T(8,128)(2,1)}, bf16[2,2816,1024]{2,1,0:T(8,128)(2,1)}, f32[8,64,2816]{2,1,0:T(8,...) custom-call(bf16[2,1024,2816]{2,1,0:T(8,128)(2,1)} %bitcast.3, ...), custom_call_target="tpu_custom_call" | custom-call | tf_op jit(solution)/shard_map/exchange/pallas_call | solution.py:353
  251.1 0.4 collective-permute-start.2
  251.5 2.3 collective-permute-start.3
  253.8 0.0 collective-permute-start.6
  253.8 0.0 copy-start.2
  253.8 0.0 copy-start.1
  253.9 0.0 copy-start
  253.9 24.0 %finish.1 = (bf16[2,1024,2816]{2,1,0:T(8,128)(2,1)}, bf16[2,1024,2816]{2,1,0:T(8,128)(2,1)}, bf16[2,2816,1024]{2,1,0:T(8,128)(2,1)}, f32[2,128,2816]{2,1,0:T(8,1...) custom-call(bf16[2,1024,2816]{2,1,0:T(8,128)(2,1)} %get-tuple-elemen, ...), custom_call_target="tpu_custom_call" | custom-call | flops 1730150400 | bytes 86507520 | tf_op jit(solution)/shard_map/finish/pallas_call | solution.py:446
  277.8 3.7 %collective-permute-done.2.refs_0_ = bf16[4,64,2816]{2,1,0:T(8,128)(2,1)S(1)} collective-permute-done((bf16[4,64,2816]{2,1,0:T(8,128)(2,1)}, bf16[4,64,2816]{2,1,0:T(8,128)(2,1)S(1)}, u32[]{:S(2)}, u32[]{:S(2)}) %collective-permute-start.2) | collective-permute-done | bytes 1441824 | tf_op jit(solution)/shard_map/ppermute | solution.py:515
  281.6 0.0 collective-permute-done.3.refs_1_
  281.6 0.0 collective-permute-start.4
  281.6 0.5 collective-permute-start.5
  282.1 0.0 copy-done.2
  282.1 0.2 collective-permute-start
  282.2 0.0 copy-done.1
  282.2 2.9 collective-permute-start.1
  285.1 0.0 collective-permute-done.6.refs_3_
  285.1 0.0 copy-done
  285.1 2.8 place_late.4
  287.9 0.0 collective-permute-done.4.refs_0_
  287.9 0.0 collective-permute-done.5.refs_1_
  287.9 1.7 place_late.5
  289.6 11.9 %collective-permute-done.refs_0_ = bf16[2,176,1024]{2,1,0:T(8,128)(2,1)S(1)} collective-permute-done((bf16[2,176,1024]{2,1,0:T(8,128)(2,1)S(1)}, bf16[2,176,1024]{2,1,0:T(8,128)(2,1)S(1)}, u32[]{:S(2)}, u32[]{:S(2)}) %collective-permute-start) | collective-permute-done | bytes 720928 | tf_op jit(solution)/shard_map/ppermute | solution.py:515
  301.5 0.0 collective-permute-done.1.refs_1_
  301.5 0.6 collective-permute-start.7
  302.1 0.0 collective-permute-start.8
  302.1 1.1 place_late.6
  303.3 0.7 collective-permute-done.7.refs_0_
  303.9 1.0 collective-permute-done.8.refs_1_
  305.0 1.1 place_late.7
Async XLA Ops:
  251.1 30.5 %collective-permute-start.2 = (bf16[4,64,2816]{2,1,0:T(8,128)(2,1)}, bf16[4,64,2816]{2,1,0:T(8,128)(2,1)S(1)}, u32[]{:S(2)}, u32[]{:S(2)}) collective-permute-start(bf16[4,64,2816]{2,1,0:T(8,128)(2,1)} %get-tuple-element.54), channel_id=1, source_target_pairs={{0,2},{1,3},{2,4},{3,5},{4,6},{5,7},{6,0},{7,1},{8,10},{9,11},{10,... | collective-permute-start | bytes 4325384 | tf_op jit(solution)/shard_map/ppermute | solution.py:515
  251.5 30.0 %collective-permute-start.3 = (bf16[4,64,2816]{2,1,0:T(8,128)(2,1)}, bf16[4,64,2816]{2,1,0:T(8,128)(2,1)S(1)}, u32[]{:S(2)}, u32[]{:S(2)}) collective-permute-start(bf16[4,64,2816]{2,1,0:T(8,128)(2,1)} %get-tuple-element.55), channel_id=1, source_target_pairs={{0,6},{1,7},{2,0},{3,1},{4,2},{5,3},{6,4},{7,5},{8,14},{9,15},{10,... | collective-permute-start | bytes 4325384 | tf_op jit(solution)/shard_map/ppermute | solution.py:515
  253.8 31.3 %collective-permute-start.6 = (bf16[4,176,1024]{2,1,0:T(8,128)(2,1)}, bf16[4,176,1024]{2,1,0:T(8,128)(2,1)S(1)}, u32[]{:S(2)}, u32[]{:S(2)}) collective-permute-start(bf16[4,176,1024]{2,1,0:T(8,128)(2,1)} %get-tuple-element.68.refs_2_), channel_id=1, source_target_pairs={{0,1},{1,0},{2,3},{3,2},{4,5},{5,4},{6,7},{7,6},{8,9},{9,8},{10,11... | collective-permute-start | bytes 4325384 | tf_op jit(solution)/shard_map/ppermute | solution.py:516
  253.8 28.2 %copy-start.2 = (bf16[2,176,1024]{2,1,0:T(8,128)(2,1)S(1)}, bf16[2,176,1024]{2,1,0:T(8,128)(2,1)}, u32[]{:S(2)}) copy-start(bf16[2,176,1024]{2,1,0:T(8,128)(2,1)} %get-tuple-element.52) | copy-start | bytes 2162692
  253.8 28.4 %copy-start.1 = (bf16[2,176,1024]{2,1,0:T(8,128)(2,1)S(1)}, bf16[2,176,1024]{2,1,0:T(8,128)(2,1)}, u32[]{:S(2)}) copy-start(bf16[2,176,1024]{2,1,0:T(8,128)(2,1)} %get-tuple-element.53) | copy-start | bytes 2162692
  253.9 31.3 %copy-start = (bf16[4,176,1024]{2,1,0:T(8,128)(2,1)S(1)}, bf16[4,176,1024]{2,1,0:T(8,128)(2,1)}, u32[]{:S(2)}) copy-start(bf16[4,176,1024]{2,1,0:T(8,128)(2,1)} %get-tuple-element.68.refs_2_) | copy-start | bytes 4325380
  281.6 6.4 %collective-permute-start.4 = (bf16[4,64,2816]{2,1,0:T(8,128)(2,1)S(1)}, bf16[4,64,2816]{2,1,0:T(8,128)(2,1)S(1)}, u32[]{:S(2)}, u32[]{:S(2)}) collective-permute-start(bf16[4,64,2816]{2,1,0:T(8,128)(2,1)S(1)} %collective-permute-done.2.refs_0_), channel_id=1, source_target_pairs={{0,1},{1,0},{2,3},{3,2},{4,5},{5,4},{6,7},{7,6},{8,9},{9,8},{10,11... | collective-permute-start | bytes 4325384 | tf_op jit(solution)/shard_map/ppermute | solution.py:523
  281.6 6.4 %collective-permute-start.5 = (bf16[4,64,2816]{2,1,0:T(8,128)(2,1)S(1)}, bf16[4,64,2816]{2,1,0:T(8,128)(2,1)S(1)}, u32[]{:S(2)}, u32[]{:S(2)}) collective-permute-start(bf16[4,64,2816]{2,1,0:T(8,128)(2,1)S(1)} %collective-permute-done.3.refs_1_), channel_id=1, source_target_pairs={{0,1},{1,0},{2,3},{3,2},{4,5},{5,4},{6,7},{7,6},{8,9},{9,8},{10,11... | collective-permute-start | bytes 4325384 | tf_op jit(solution)/shard_map/ppermute | solution.py:523
  282.1 19.5 %collective-permute-start = (bf16[2,176,1024]{2,1,0:T(8,128)(2,1)S(1)}, bf16[2,176,1024]{2,1,0:T(8,128)(2,1)S(1)}, u32[]{:S(2)}, u32[]{:S(2)}) collective-permute-start(bf16[2,176,1024]{2,1,0:T(8,128)(2,1)S(1)} %copy-done.2), channel_id=1, source_target_pairs={{0,2},{1,3},{2,4},{3,5},{4,6},{5,7},{6,0},{7,1},{8,10},{9,11},{10,... | collective-permute-start | bytes 2162696 | tf_op jit(solution)/shard_map/ppermute | solution.py:515
  282.2 19.3 %collective-permute-start.1 = (bf16[2,176,1024]{2,1,0:T(8,128)(2,1)S(1)}, bf16[2,176,1024]{2,1,0:T(8,128)(2,1)S(1)}, u32[]{:S(2)}, u32[]{:S(2)}) collective-permute-start(bf16[2,176,1024]{2,1,0:T(8,128)(2,1)S(1)} %copy-done.1), channel_id=1, source_target_pairs={{0,6},{1,7},{2,0},{3,1},{4,2},{5,3},{6,4},{7,5},{8,14},{9,15},{10,... | collective-permute-start | bytes 2162696 | tf_op jit(solution)/shard_map/ppermute | solution.py:515
  301.5 2.4 collective-permute-start.7
  302.1 2.8 collective-permute-start.8

commit v4 on v3

v4 whole, which is shorter than its diff:
```python
import functools

import jax
import jax.numpy as jnp
from jax import lax
from jax.experimental import pallas as pl
from jax.experimental.pallas import tpu as pltpu
from jax.sharding import PartitionSpec as P


AXIS = "dp"
CORES = 2
AHEAD = 6
GROUP = 16
RING = 8
SLOTS, DEPTH = 16, 8
A, B, C, OWN = 0, 2, 4, 6


def adamw(w, m, v, g):
    m = 0.9 * m + 0.1 * g
    v = 0.95 * v + 0.05 * g * g
    step = m * lax.rsqrt(v + 1e-8) + 0.1 * w
    return (w - 0.02 * step).astype(jnp.bfloat16), m, v


class Places:
    def __init__(self, n, shapes):
        self.n = n
        self.layers = shapes[0][0]
        self.half = [rows // n // 2 for _, rows, _ in shapes]
        self.piece = [(h, cols) for h, (_, _, cols) in zip(self.half, shapes)]
        self.count = len(shapes) * self.layers
        self.kinds = sorted(set(self.piece), key=self.piece.index)
        self.members = [[p for p in range(self.count) if self.piece[p // self.layers] == k] for k in self.kinds]

        self.end = self.count - 1
        self.groups = [*self.members[:-1], self.members[-1][:-1], [self.end]]

    def scratch(self, slots, dtype):
        return [pltpu.VMEM((len(m) * slots, *k), dtype) for m, k in zip(self.members, self.kinds)]

    def spot(self, p):
        kind = self.kinds.index(self.piece[p // self.layers])
        return kind, self.members[kind].index(p)

    def at(self, buffers, slots, p, slot):
        kind, j = self.spot(p)
        return buffers[kind].at[j * slots + slot]

    def rows(self, refs, p, block, half):
        w = p // self.layers
        start = pl.multiple_of((block * 2 + half) * self.half[w], GROUP)
        return refs[w].at[p % self.layers, pl.ds(start, self.half[w]), :]

    def own(self, refs, p, half):
        w = p // self.layers
        return refs[w].at[p % self.layers, pl.ds(half * self.half[w], self.half[w]), :]


def exchange(places, count, *refs):
    nk = len(places.kinds)
    names = (3, 3, 3, 3, 3, nk, nk, 1, 2 * len(places.groups) + 1, nk, nk, nk, nk, *(1,) * 10)
    parts, i = [], 0
    for size in names:
        parts.append(refs[i : i + size])
        i += size
    g, w, m, v, whole, mm, vv, (factor_ref,), (*tails, last) = parts[:9]
    own, par, got, ww = parts[9:13]
    (sq,), (own_sem,), (first_sem,), (par_recv,), (came_sem,), (pass_sem,), (all_sem,), (extra_send,), (extra_recv,), (end_recv,) = parts[13:]

    n, at, end = places.n, places.at, places.end
    chips = n // CORES
    me = lax.axis_index(AXIS)
    core, chip = lax.rem(me, CORES), lax.div(me, CORES)
    away = lambda k, core: lax.rem(chip + (k + chips), chips) * CORES + core
    partner = away(0, 1 - core)
    sign = (1, -1)
    beside = [away(s, core) for s in sign]
    second = core == CORES - 1
    kind_of = lambda p: places.spot(p)[0]
    each = range(nk)

    def remote(src, dst, send, recv, device):
        return pltpu.make_async_remote_copy(
            src_ref=src, dst_ref=dst, send_sem=send, recv_sem=recv, device_id={AXIS: device}, device_id_type=pl.DeviceIdType.MESH
        )

    SUM_GIVEN, SUM_A, SUM_B, SUM_C, B_CAME, M, V, W, SENT, ACROSS, ACROSS_CAME, KEPT, HANDED, TOLD, HEARD = range(15)
    shared = lambda what, p: all_sem.at[what, kind_of(p)]

    def all_of(what, kind, ref, size):
        sem, ref = all_sem.at[what, kind], ref if size is None else ref.at[pl.ds(0, size)]
        remote(ref, ref, sem, sem, partner).wait_recv()

    def place(kind):
        i = kind % 2
        if kind < B:
            return 2, 1 - i, i
        if kind < C:
            return sign[i], i, 2 + i
        if kind < OWN:
            return sign[i], 1 - i, i
        return 0, i, 3 - i

    spots = range(places.count)
    steps = [(k + i, p) for k in (A, B, C) for p in spots for i in range(2)] + [(OWN + h, p) for p in spots for h in (1, 0)]
    groups = lambda p: places.half[p // places.layers] // GROUP
    part = lambda ref, r: ref if r is None else ref.at[pl.ds(r * GROUP, GROUP), :]

    def load(t):
        kind, p = steps[t]
        to, half, slot = place(kind)
        return pltpu.make_async_copy(places.rows(g, p, away(to, core), half), at(own, 4, p, slot), own_sem.at[t % RING])

    def give(t, r=None):
        kind, p = steps[t]
        to, half, _ = place(kind)
        recv = par_recv.at[t % (2 * RING)] if r is None else first_sem.at[t, r]
        src, dst = part(places.rows(g, p, away(to, 1 - core), half), r), part(at(par, 8, p, kind), r)
        return remote(src, dst, shared(SUM_GIVEN, p), recv, partner)

    def send(kind, p, r=None):
        what, i = (SUM_A, SUM_B, SUM_C)[kind // 2], kind % 2
        recv = (came_sem.at[p, i], shared(B_CAME, p), pass_sem.at[p, i])[kind // 2]
        return remote(part(at(own, 4, p, place(kind)[2]), r), part(at(got, 6, p, kind), r), shared(what, p), recv, beside[i])

    def start_load(t):
        if steps[t] in ((C, 0), (OWN + 1, 0)):
            for k in each:
                all_of(SUM_A if steps[t][0] < OWN else SUM_B, k, own[k], 2 * len(places.members[k]))
        load(t).start()

    def add_up(kind, p, first, last):
        out = at(own, 4, p, place(kind)[2])
        terms = [out, at(par, 8, p, kind)]
        if C <= kind < OWN:
            terms.append(at(got, 6, p, kind - C))
        if kind >= OWN:
            i = 1 - (kind - OWN)
            terms += [at(got, 6, p, C + i), at(got, 6, p, B + 1 - i)]

        def body(r, carry):
            rows = pl.ds(pl.multiple_of(r * GROUP, GROUP), GROUP)
            total = terms[0][rows, :].astype(jnp.float32)
            for one in terms[1:]:
                total = total + one[rows, :].astype(jnp.float32)
            total = total.astype(jnp.bfloat16)
            out[rows, :] = total
            if kind >= OWN:
                total = total.astype(jnp.float32)
                total = total * total
                tiles = [total[a : a + 8, b : b + 128] for a in range(0, GROUP, 8) for b in range(0, total.shape[1], 128)]
                sums = [sum(tiles[j::4]) for j in range(4)]
                carry = carry + ((sums[0] + sums[1]) + (sums[2] + sums[3]))
            return carry

        if kind < OWN:
            lax.fori_loop(first, last, body, 0)
        else:
            sq[me] = lax.fori_loop(first, last, body, sq[me])

    for t in range(AHEAD):
        start_load(t)
    barrier = pltpu.get_barrier_semaphore()
    for device in (partner, *beside):
        pl.semaphore_signal(barrier, inc=1, device_id={AXIS: device}, device_id_type=pl.DeviceIdType.MESH)
    pl.semaphore_wait(barrier, 3)
    for r in range(groups(0)):
        for t in range(2):
            give(t, r).start()
    for t in range(2, AHEAD):
        give(t).start()
    sq[me] = jnp.zeros(sq.shape[1:], jnp.float32)

    for r in range(groups(0)):
        for t in range(2):
            if r == 0:
                load(t).wait()
            give(t, r).wait_recv()
            add_up(*steps[t], r, r + 1)
            send(*steps[t], r).start()
    for t, (kind, p) in enumerate(steps):
        if t + AHEAD < len(steps):
            give(t + AHEAD).start()
        if t >= 2:
            load(t).wait()
            give(t).wait_recv()
            if C <= kind < OWN:
                send(kind - C, p).wait_recv()
            if (kind, p) == (OWN + 1, 0):
                for k in each:
                    all_of(B_CAME, k, got[k], 2 * len(places.members[k]))
            if kind >= OWN:
                send(C + 1 - (kind - OWN), p).wait_recv()
            add_up(kind, p, 0, groups(p))
            if kind < OWN:
                send(kind, p).start()
        if t + AHEAD < len(steps):
            start_load(t + AHEAD)
        if t == 2 * places.count:
            for q in spots:
                for h in range(2):
                    pltpu.make_async_copy(places.own(m, q, h), at(mm, 2, q, h), shared(M, q)).start()
                    pltpu.make_async_copy(places.own(v, q, h), at(vv, 2, q, h), shared(V, q)).start()
                    pltpu.make_async_copy(places.rows(w, q, me, h), at(ww, 2, q, h), shared(W, q)).start()

    for o in range(1, n):
        remote(sq.at[me], sq.at[me], all_sem.at[TOLD, 0], all_sem.at[HEARD, 0], lax.rem(me + o, n)).start()
    for k in each:
        all_of(SUM_C, k, own[k], 2 * len(places.members[k]))
        all_of(SUM_GIVEN, k, par[k], None)
        for what, buffers in ((M, mm), (V, vv), (W, ww)):
            all_of(what, k, buffers[k], None)
    all_of(HEARD, 0, sq, n - 1)
    total = sq[0]
    for d in range(1, n):
        total = total + sq[d]
    total = jnp.full(factor_ref.shape, jnp.sum(total), jnp.float32)
    factor_ref[...] = jnp.minimum(1.0, 0.5 * lax.rsqrt(total / count + 1e-30))

    def ahead(i, p, h, r=None):
        there = part(places.rows(whole, p, me, h), r)
        return remote(part(at(ww, 2, p, h), r), there, shared(SENT, p), came_sem.at[p, i], beside[i])

    def ahead_came(i, p):
        here = places.rows(whole, p, away(-sign[i], core), 1 - i)
        return remote(here, here, shared(SENT, p), came_sem.at[p, i], beside[i])

    def onward(i, p):
        here = places.rows(whole, p, away(-sign[i], core), 1 - i)
        if p == end:
            return remote(here, last.at[i], extra_send.at[i], pass_sem.at[p, i], beside[i])
        return remote(here, here, shared(SENT, p), pass_sem.at[p, i], beside[i])

    def onward_came(i, p):
        here = places.rows(whole, p, away(2, core), 1 - i)
        return remote(here, here, shared(SENT, p), pass_sem.at[p, i], beside[i])

    def extra(i):
        here = places.rows(whole, end, away(-sign[i], 1 - core), 1 - i)
        return remote(here, last.at[2 + i], extra_send.at[2 + i], extra_recv.at[i], beside[i])

    def across(k, p):
        if k < 2:
            here = places.rows(whole, p, away(-sign[k], core), 1 - k)
        elif k < 4:
            here = places.rows(whole, p, away(2, core), 1 - (k - 2))
        else:
            here = places.rows(whole, p, me, k - 4)
        src = here if k < 4 else at(ww, 2, p, k - 4)
        recv = end_recv.at[k] if p == end and k < 2 else shared(ACROSS_CAME, p)
        return remote(src, here, shared(ACROSS, p), recv, partner)

    def side_came_across(i):
        here = places.rows(whole, end, away(-sign[i], 1 - core), 1 - i)
        return remote(here, here, end_recv.at[i], end_recv.at[i], partner)

    def update(p, h, first, last):
        gs, ms, vs, ws = at(own, 4, p, 3 - h), at(mm, 2, p, h), at(vv, 2, p, h), at(ww, 2, p, h)

        def body(r, carry):
            rows = pl.ds(pl.multiple_of(r * GROUP, GROUP), GROUP)
            grad = gs[rows, :].astype(jnp.float32) * factor_ref[0:1, 0:1]
            ws[rows, :], ms[rows, :], vs[rows, :] = adamw(ws[rows, :].astype(jnp.float32), ms[rows, :], vs[rows, :], grad)
            return carry

        lax.fori_loop(first, last, body, 0)

    for r in range(groups(0)):
        for h in (1, 0):
            update(0, h, r, r + 1)
            ahead(1 - h, 0, h, r).start()
    for p in spots:
        for h in (1, 0):
            if p:
                update(p, h, 0, groups(p))
                ahead(1 - h, p, h).start()
            across(4 + h, p).start()
            pltpu.make_async_copy(at(ww, 2, p, h), places.rows(whole, p, me, h), shared(KEPT, p)).start()
            k, j = next((k, one.index(p)) for k, one in enumerate(places.groups) if p in one)
            pltpu.make_async_copy(at(ww, 2, p, h), tails[2 * k + h].at[j], shared(HANDED, p)).start()
    for p in spots:
        for i in range(2):
            ahead_came(i, p).wait_recv()
            if p != end:
                onward(i, p).start()
            across(i, p).start()

    @pl.when(second)
    def _():
        for i in range(2):
            onward(i, end).start()
        for i in range(2):
            side_came_across(i).wait_recv()
            extra(i).start()

    for p in spots[:-1]:
        for i in range(2):
            onward_came(i, p).wait_recv()
            across(2 + i, p).start()
    for k in each:
        members = len(places.members[k])
        ends = 1 if k == kind_of(end) else 0
        all_of(SENT, k, own[k], 4 * members - 2 * ends)
        all_of(ACROSS, k, par[k], 6 * members - 2 * ends)
        all_of(ACROSS_CAME, k, par[k], 6 * members - 4 * ends)
        all_of(KEPT, k, ww[k], None)
        all_of(HANDED, k, ww[k], None)
    all_of(TOLD, 0, sq, n - 1)

    @pl.when(second)
    def _():
        for i in range(2):
            for copy in (onward(i, end), extra(i)):
                copy.wait()

    @pl.when(jnp.logical_not(second))
    def _():
        for i in range(2):
            side_came_across(i).wait_recv()


def gather_new(terms, weights, m, v, n):
    shapes = [w.shape for w in weights]
    places = Places(n, shapes)
    count = float(sum(w.size for w in weights))
    anywhere, vmem = pl.BlockSpec(memory_space=pl.ANY), pl.BlockSpec(memory_space=pltpu.VMEM)
    out = [pltpu.HBM(s, jnp.bfloat16) for s in shapes]
    out += places.scratch(2, jnp.float32) * 2
    out += [jax.ShapeDtypeStruct((8, 128), jnp.float32)]
    out += [jax.ShapeDtypeStruct((len(one), *places.piece[one[0] // places.layers]), jnp.bfloat16) for one in places.groups for _ in range(2)]
    out += [jax.ShapeDtypeStruct((4, *places.piece[-1]), jnp.bfloat16)]
    dma = pltpu.SemaphoreType.DMA
    half, nk = jnp.bfloat16, len(places.kinds)
    scratch = [
        *places.scratch(4, half), *places.scratch(8, half), *places.scratch(6, half),
        *places.scratch(2, half),
        pltpu.VMEM((n, 8, 128), jnp.float32),
        dma((RING,)), dma((2, places.half[0] // GROUP)), dma((2 * RING,)), dma((places.count, 2)), dma((places.count, 2)),
        dma((15, nk)), dma((4,)), dma((2,)), dma((2,)),
    ]
    got = pl.pallas_call(
        functools.partial(exchange, places, count),
        out_shape=out,
        in_specs=[anywhere] * 12,
        out_specs=[anywhere] * 3 + [vmem] * (2 * nk + 1) + [anywhere] * (2 * len(places.groups) + 1),
        scratch_shapes=scratch,
        compiler_params=pltpu.CompilerParams(collective_id=0, has_side_effects=True, vmem_limit_bytes=46 * 1000 * 1000),
        name="exchange",
    )(*terms, *weights, *m, *v)
    got_m, got_v, rest = got[3 : 3 + nk], got[3 + nk : 3 + 2 * nk], got[4 + 2 * nk :]
    return got[:3], got_m, got_v, rest[:-1], rest[-1]


def params(**more):
    return pltpu.CompilerParams(has_side_effects=False, **more)


def finish(places, tail, *refs):
    nk = len(places.kinds)
    parts, i = [], 0
    for size in (3, nk, nk, 3, 3, 3, nk, 1, 1, 1):
        parts.append(refs[i : i + size])
        i += size
    whole, mm, vv, out, new_m, new_v, slots, (in_sem,), (out_sem,), (put_sem,) = parts
    n = places.n
    chips = n // CORES
    chip = lax.div(lax.axis_index(AXIS), CORES)
    pieces = [(p, h) for p in range(places.count) for h in range(2)]

    def puts(p, h):
        refs = ((mm, new_m), (vv, new_v))
        return [pltpu.make_async_copy(places.at(a, 2, p, h), places.own(b, p, h), put_sem.at[j, places.spot(p)[0]]) for j, (a, b) in enumerate(refs)]

    items = []
    for p, h in pieces:
        for k in range(chips):
            if p in tail and k == (1 if h else chips - 1) or p == places.end and k == 2:
                continue
            items += [(p, h, k, c) for c in range(CORES)]
    turn, of_kind = [], [[] for _ in range(nk)]
    for t, (p, *_) in enumerate(items):
        kind, _ = places.spot(p)
        turn.append((kind, len(of_kind[kind])))
        of_kind[kind].append(t)

    def ends(t):
        p, h, k, c = items[t]
        block = lax.rem(chip + k, chips) * CORES + c
        kind, u = turn[t]
        return places.rows(whole, p, block, h), slots[kind].at[u % SLOTS], places.rows(out, p, block, h), (kind, u % SLOTS)

    def read(t):
        src, slot, _, sem = ends(t)
        return pltpu.make_async_copy(src, slot, in_sem.at[sem])

    def write(t):
        _, slot, dst, sem = ends(t)
        return pltpu.make_async_copy(slot, dst, out_sem.at[sem])

    def start_read(t):
        kind, u = turn[t]
        if u >= SLOTS:
            write(of_kind[kind][u - SLOTS]).wait()
        read(t).start()

    for t in range(min(DEPTH, len(items))):
        start_read(t)
    done = 0
    for t in range(len(items)):
        read(t).wait()
        write(t).start()
        if t + DEPTH < len(items):
            start_read(t + DEPTH)
        while done * len(items) < (t + 1) * len(pieces) and done < len(pieces):
            for copy in puts(*pieces[done]):
                copy.start()
            done += 1
    for kind in range(nk):
        for t in of_kind[kind][-SLOTS:]:
            write(t).wait()
    for kind in range(nk):
        for j, one in enumerate((mm, vv)):
            pltpu.make_async_copy(one[kind], one[kind], put_sem.at[j, kind]).wait()


def finish_all(places, tail, whole, mm, vv, m, v):
    anywhere, vmem = pl.BlockSpec(memory_space=pl.ANY), pl.BlockSpec(memory_space=pltpu.VMEM)
    dma = pltpu.SemaphoreType.DMA
    nk = len(places.kinds)
    size = sum(w.size for w in whole)
    mine = sum(one.size for one in m)
    whole = [pltpu.with_memory_space_constraint(w, pltpu.HBM) for w in whole]
    mm, vv = ([pltpu.with_memory_space_constraint(one, pltpu.VMEM) for one in x] for x in (mm, vv))
    return pl.pallas_call(
        functools.partial(finish, places, tail),
        out_shape=[jax.ShapeDtypeStruct(a.shape, a.dtype) for a in (*whole, *m, *v)],
        in_specs=[anywhere] * 3 + [vmem] * (2 * nk),
        out_specs=[anywhere] * 9,
        scratch_shapes=[
            *(pltpu.VMEM((SLOTS, *k), jnp.bfloat16) for k in places.kinds),
            dma((nk, SLOTS)), dma((nk, SLOTS)), dma((2, nk)),
        ],
        compiler_params=params(vmem_limit_bytes=24 * 1024 * 1024),
        cost_estimate=pl.CostEstimate(flops=size * 100, bytes_accessed=size * 4 + mine * 8, transcendentals=0),
        name="finish",
    )(*whole, *mm, *vv)


def place_late(places, spots, *refs):
    k = len(spots)
    arrays, out, sem = refs[:k], refs[k + 3 : k + 6], refs[k + 6]
    chips = places.n // CORES
    me = lax.axis_index(AXIS)
    core, chip = lax.rem(me, CORES), lax.div(me, CORES)
    jobs = {}
    for array, (only, pieces) in zip(arrays, spots):
        for j, (p, h, away, which) in enumerate(pieces):
            block = lax.rem(chip + (away + chips), chips) * CORES + (lax.rem(core + which[1], CORES) if which[0] else which[1])
            mine = jobs.setdefault(only, [])
            mine.append(pltpu.make_async_copy(array.at[j], places.rows(out, p, block, h), sem.at[sum(len(x) for x in jobs.values())]))

    for only, copies in jobs.items():

        def run():
            for copy in copies:
                copy.start()
            for copy in copies:
                copy.wait()

        run() if only is None else pl.when(core == only)(run)


def place_all(places, spots, arrays, out):
    anywhere, vmem = pl.BlockSpec(memory_space=pl.ANY), pl.BlockSpec(memory_space=pltpu.VMEM)
    k = len(spots)
    return pl.pallas_call(
        functools.partial(place_late, places, spots),
        out_shape=[jax.ShapeDtypeStruct(w.shape, w.dtype) for w in out],
        in_specs=[vmem] * k + [anywhere] * 3,
        out_specs=[anywhere] * 3,
        input_output_aliases={k + j: j for j in range(3)},
        scratch_shapes=[pltpu.SemaphoreType.DMA((sum(len(one) for _, one in spots),))],
        compiler_params=params(vmem_limit_bytes=16 * 1024 * 1024),
        cost_estimate=pl.CostEstimate(flops=10**7, bytes_accessed=sum(x.size for x in arrays) * 4, transcendentals=0),
        name="place_late",
    )(*arrays, *out)


def solution(mesh):
    n = mesh.shape[AXIS]
    chips = n // CORES

    def step(*arrays):
        terms, weights, m, v = (arrays[i : i + 3] for i in (0, 3, 6, 9))
        places = Places(n, [w.shape for w in weights])
        tail = list(range(places.count))
        whole, mm, vv, late, last = gather_new([t[0] for t in terms], weights, m, v, n)
        groups = range(len(places.groups))
        shift = [[(j, (j // CORES + s) % chips * CORES + j % CORES) for j in range(n)] for s in (1, -1)]
        swap = [(j, j // CORES * CORES + (CORES - 1 - j % CORES)) for j in range(n)]
        came = []
        for k in groups:
            came.append([lax.ppermute(late[2 * k + h], AXIS, shift[h]) for h in range(2)])
        last_swapped = lax.ppermute(last, AXIS, swap)
        *out, m0, m1, m2, v0, v1, v2 = finish_all(places, tail, whole, mm, vv, m, v)
        own, other = (True, 0), (True, 1)
        spots = lambda k, which: [(None, [(p, h, -1 if h == 0 else 1, which) for p in places.groups[k]]) for h in range(2)]
        ends = [(places.end, 1 - i, 2, (False, c)) for c in (1, 0) for i in range(2)]
        for k in groups:
            here, out = lax.optimization_barrier((came[k], out))
            swapped = [lax.ppermute(piece, AXIS, swap) for piece in here]
            if k == 0:
                out = place_all(places, [*spots(k, own), (1, ends), (0, ends)], [*here, last, last_swapped], out)
            else:
                out = place_all(places, spots(k, own), here, out)
            out = place_all(places, spots(k, other), swapped, out)
        return (*out, m0, m1, m2, v0, v1, v2)

    all_of, cut = P(None, None, None), P(None, AXIS, None)
    return jax.shard_map(
        step,
        mesh=mesh,
        in_specs=(P(("rep", AXIS), None, None, None),) * 3 + (all_of,) * 3 + (cut,) * 6,
        out_specs=(P("rep", None, None),) * 3 + (P("rep", AXIS, None),) * 6,
        check_vma=False,
    )
```

time: 306 us -> 307 us (level)
  starting transfers between devices: 6.89 us -> 11 us
    ppermute x4 -> x6, starting transfers between devices: 5.79 us -> 8.63 us  [step(): lax.ppermute(late[2 * k + h], AXIS, shift[h])]
    pallas_call x4 -> x6, Pallas kernels: 6.7 us -> 7.95 us  [place_all(): pl.pallas_call(functools.partial(place_late, places, spots), out_shape=[j...]
    ppermute x4 -> x6, waiting for transfers between devices: 15.7 us -> 15.4 us  [step(): lax.ppermute(late[2 * k + h], AXIS, shift[h])]
  transfers between devices with their start and end apart: 9 -> 13, of which waited for: 4 -> 5; matrix products, arithmetic and copies ran while one was open for 0% -> 0% of each run, Pallas kernels for 10% -> 10%
where the time goes in v4:
time: 307 us
  Pallas kernels  279 us (91%)
  waiting for transfers between devices  16.3 us (5%)
  starting transfers between devices  11 us (4%)
    pallas_call x1, Pallas kernels, gather_new(): pl.pallas_call(functools.partial(exchange, places, count), out_shape=out,...  248 us
    pallas_call x1, Pallas kernels, finish_all(): pl.pallas_call(functools.partial(finish, places, tail), out_shape=[jax.Sh...  23.2 us
    ppermute x6, waiting for transfers between devices, step(): lax.ppermute(late[2 * k + h], AXIS, shift[h])  15.4 us
    ppermute x6, starting transfers between devices, step(): lax.ppermute(late[2 * k + h], AXIS, shift[h])  8.63 us
    pallas_call x6, Pallas kernels, place_all(): pl.pallas_call(functools.partial(place_late, places, spots), out_shape=[j...  7.95 us
  transfers between devices with their start and end apart: 13, of which 5 were waited for; matrix products, arithmetic and copies ran while one was open for 0% of the time, Pallas kernels for 10%

profile of v4, /device:TPU:113, one launch (start us, length us, event | category | flops | bytes accessed | tf_op | source)
XLA Modules:
  0.0 306.8 jit_solution(407747131688349953)
XLA Ops:
  0.6 247.6 %exchange.1 = (bf16[2,1024,2816]{2,1,0:T(8,128)(2,1)}, bf16[2,1024,2816]{2,1,0:T(8,128)(2,1)}, bf16[2,2816,1024]{2,1,0:T(8,128)(2,1)}, f32[8,64,2816]{2,1,0:T(8,...) custom-call(bf16[2,1024,2816]{2,1,0:T(8,128)(2,1)} %bitcast.3, ...), custom_call_target="tpu_custom_call" | custom-call | tf_op jit(solution)/shard_map/exchange/pallas_call | solution.py:343
  248.2 0.1 collective-permute-start.4
  248.3 2.6 collective-permute-start.5
  251.0 0.0 collective-permute-start.8
  251.0 23.2 %finish.1 = (bf16[2,1024,2816]{2,1,0:T(8,128)(2,1)}, bf16[2,1024,2816]{2,1,0:T(8,128)(2,1)}, bf16[2,2816,1024]{2,1,0:T(8,128)(2,1)}, f32[2,128,2816]{2,1,0:T(8,1...) custom-call(bf16[2,1024,2816]{2,1,0:T(8,128)(2,1)} %get-tuple-elemen, ...), custom_call_target="tpu_custom_call" | custom-call | flops 1730150400 | bytes 86507520 | tf_op jit(solution)/shard_map/finish/pallas_call | solution.py:436
  274.2 5.0 %collective-permute-done.4.refs_0_ = bf16[4,64,2816]{2,1,0:T(8,128)(2,1)S(1)} collective-permute-done((bf16[4,64,2816]{2,1,0:T(8,128)(2,1)}, bf16[4,64,2816]{2,1,0:T(8,128)(2,1)S(1)}, u32[]{:S(2)}, u32[]{:S(2)}) %collective-permute-start.4) | collective-permute-done | bytes 1441824 | tf_op jit(solution)/shard_map/ppermute | solution.py:505
  279.2 0.0 collective-permute-done.5.refs_1_
  279.2 0.0 collective-permute-start.6
  279.2 0.5 collective-permute-start.7
  279.7 0.0 collective-permute-start.2
  279.7 3.0 collective-permute-start.3
  282.7 0.0 collective-permute-done.8.refs_3_
  282.7 2.8 place_late.6
  285.5 0.0 collective-permute-done.6.refs_0_
  285.6 0.0 collective-permute-done.7.refs_1_
  285.6 1.7 place_late.7
  287.3 4.2 %collective-permute-done.2.refs_0_ = bf16[1,176,1024]{2,1,0:T(8,128)(2,1)S(1)} collective-permute-done((bf16[1,176,1024]{2,1,0:T(8,128)(2,1)S(1)}, bf16[1,176,1024]{2,1,0:T(8,128)(2,1)S(1)}, u32[]{:S(2)}, u32[]{:S(2)}) %collective-permute-start.2) | collective-permute-done | bytes 360480 | tf_op jit(solution)/shard_map/ppermute | solution.py:505
  291.4 0.0 collective-permute-done.3.refs_1_
  291.4 0.6 collective-permute-start.10
  292.0 0.0 collective-permute-start.9
  292.0 0.9 collective-permute-start
  292.9 2.0 collective-permute-start.1
  294.9 0.9 place_late.8
  295.8 0.0 collective-permute-done.10.refs_1_
  295.8 0.9 place_late.9
  296.7 6.2 %collective-permute-done.refs_0_ = bf16[1,176,1024]{2,1,0:T(8,128)(2,1)S(1)} collective-permute-done((bf16[1,176,1024]{2,1,0:T(8,128)(2,1)S(1)}, bf16[1,176,1024]{2,1,0:T(8,128)(2,1)S(1)}, u32[]{:S(2)}, u32[]{:S(2)}) %collective-permute-start) | collective-permute-done | bytes 360480 | tf_op jit(solution)/shard_map/ppermute | solution.py:505
  302.9 1.3 collective-permute-start.11
  304.2 0.0 collective-permute-start.12
  304.2 0.9 place_late.10
  305.0 0.4 collective-permute-done.11.refs_0_
  305.5 0.5 collective-permute-done.12.refs_1_
  306.0 0.9 place_late.11
  (12 shorter events, 0.0 us)
Async XLA Ops:
  248.2 31.0 %collective-permute-start.4 = (bf16[4,64,2816]{2,1,0:T(8,128)(2,1)}, bf16[4,64,2816]{2,1,0:T(8,128)(2,1)S(1)}, u32[]{:S(2)}, u32[]{:S(2)}) collective-permute-start(bf16[4,64,2816]{2,1,0:T(8,128)(2,1)} %get-tuple-element.69), channel_id=1, source_target_pairs={{0,2},{1,3},{2,4},{3,5},{4,6},{5,7},{6,0},{7,1},{8,10},{9,11},{10,... | collective-permute-start | bytes 4325384 | tf_op jit(solution)/shard_map/ppermute | solution.py:505
  248.3 30.9 %collective-permute-start.5 = (bf16[4,64,2816]{2,1,0:T(8,128)(2,1)}, bf16[4,64,2816]{2,1,0:T(8,128)(2,1)S(1)}, u32[]{:S(2)}, u32[]{:S(2)}) collective-permute-start(bf16[4,64,2816]{2,1,0:T(8,128)(2,1)} %get-tuple-element.70), channel_id=1, source_target_pairs={{0,6},{1,7},{2,0},{3,1},{4,2},{5,3},{6,4},{7,5},{8,14},{9,15},{10,... | collective-permute-start | bytes 4325384 | tf_op jit(solution)/shard_map/ppermute | solution.py:505
  251.0 31.8 %collective-permute-start.8 = (bf16[4,176,1024]{2,1,0:T(8,128)(2,1)}, bf16[4,176,1024]{2,1,0:T(8,128)(2,1)S(1)}, u32[]{:S(2)}, u32[]{:S(2)}) collective-permute-start(bf16[4,176,1024]{2,1,0:T(8,128)(2,1)} %get-tuple-element.83.refs_2_), channel_id=1, source_target_pairs={{0,1},{1,0},{2,3},{3,2},{4,5},{5,4},{6,7},{7,6},{8,9},{9,8},{10,11... | collective-permute-start | bytes 4325384 | tf_op jit(solution)/shard_map/ppermute | solution.py:506
  251.0 28.7 %copy-start.4 = (bf16[1,176,1024]{2,1,0:T(8,128)(2,1)S(1)}, bf16[1,176,1024]{2,1,0:T(8,128)(2,1)}, u32[]{:S(2)}) copy-start(bf16[1,176,1024]{2,1,0:T(8,128)(2,1)} %get-tuple-element.67) | copy-start | bytes 1081348
  251.0 28.7 %copy-start.3 = (bf16[1,176,1024]{2,1,0:T(8,128)(2,1)S(1)}, bf16[1,176,1024]{2,1,0:T(8,128)(2,1)}, u32[]{:S(2)}) copy-start(bf16[1,176,1024]{2,1,0:T(8,128)(2,1)} %get-tuple-element.68) | copy-start | bytes 1081348
  251.0 31.8 %copy-start = (bf16[4,176,1024]{2,1,0:T(8,128)(2,1)S(1)}, bf16[4,176,1024]{2,1,0:T(8,128)(2,1)}, u32[]{:S(2)}) copy-start(bf16[4,176,1024]{2,1,0:T(8,128)(2,1)} %get-tuple-element.83.refs_2_) | copy-start | bytes 4325380
  279.2 6.4 %collective-permute-start.6 = (bf16[4,64,2816]{2,1,0:T(8,128)(2,1)S(1)}, bf16[4,64,2816]{2,1,0:T(8,128)(2,1)S(1)}, u32[]{:S(2)}, u32[]{:S(2)}) collective-permute-start(bf16[4,64,2816]{2,1,0:T(8,128)(2,1)S(1)} %collective-permute-done.4.refs_0_), channel_id=1, source_target_pairs={{0,1},{1,0},{2,3},{3,2},{4,5},{5,4},{6,7},{7,6},{8,9},{9,8},{10,11... | collective-permute-start | bytes 4325384 | tf_op jit(solution)/shard_map/ppermute | solution.py:513
  279.2 6.4 %collective-permute-start.7 = (bf16[4,64,2816]{2,1,0:T(8,128)(2,1)S(1)}, bf16[4,64,2816]{2,1,0:T(8,128)(2,1)S(1)}, u32[]{:S(2)}, u32[]{:S(2)}) collective-permute-start(bf16[4,64,2816]{2,1,0:T(8,128)(2,1)S(1)} %collective-permute-done.5.refs_1_), channel_id=1, source_target_pairs={{0,1},{1,0},{2,3},{3,2},{4,5},{5,4},{6,7},{7,6},{8,9},{9,8},{10,11... | collective-permute-start | bytes 4325384 | tf_op jit(solution)/shard_map/ppermute | solution.py:513
  279.7 11.7 %collective-permute-start.2 = (bf16[1,176,1024]{2,1,0:T(8,128)(2,1)S(1)}, bf16[1,176,1024]{2,1,0:T(8,128)(2,1)S(1)}, u32[]{:S(2)}, u32[]{:S(2)}) collective-permute-start(bf16[1,176,1024]{2,1,0:T(8,128)(2,1)S(1)} %copy-done.4), channel_id=1, source_target_pairs={{0,2},{1,3},{2,4},{3,5},{4,6},{5,7},{6,0},{7,1},{8,10},{9,11},{10,... | collective-permute-start | bytes 1081352 | tf_op jit(solution)/shard_map/ppermute | solution.py:505
  279.7 11.7 %collective-permute-start.3 = (bf16[1,176,1024]{2,1,0:T(8,128)(2,1)S(1)}, bf16[1,176,1024]{2,1,0:T(8,128)(2,1)S(1)}, u32[]{:S(2)}, u32[]{:S(2)}) collective-permute-start(bf16[1,176,1024]{2,1,0:T(8,128)(2,1)S(1)} %copy-done.3), channel_id=1, source_target_pairs={{0,6},{1,7},{2,0},{3,1},{4,2},{5,3},{6,4},{7,5},{8,14},{9,15},{10,... | collective-permute-start | bytes 1081352 | tf_op jit(solution)/shard_map/ppermute | solution.py:505
  285.6 6.5 %copy-start.2 = (bf16[1,176,1024]{2,1,0:T(8,128)(2,1)S(1)}, bf16[1,176,1024]{2,1,0:T(8,128)(2,1)}, u32[]{:S(2)}) copy-start(bf16[1,176,1024]{2,1,0:T(8,128)(2,1)} %get-tuple-element.65) | copy-start | bytes 1081348
  285.6 7.3 %copy-start.1 = (bf16[1,176,1024]{2,1,0:T(8,128)(2,1)S(1)}, bf16[1,176,1024]{2,1,0:T(8,128)(2,1)}, u32[]{:S(2)}) copy-start(bf16[1,176,1024]{2,1,0:T(8,128)(2,1)} %get-tuple-element.66) | copy-start | bytes 1081348
  291.4 4.3 %collective-permute-start.10 = (bf16[1,176,1024]{2,1,0:T(8,128)(2,1)S(1)}, bf16[1,176,1024]{2,1,0:T(8,128)(2,1)S(1)}, u32[]{:S(2)}, u32[]{:S(2)}) collective-permute-start(bf16[1,176,1024]{2,1,0:T(8,128)(2,1)S(1)} %collective-permute-done.3.refs_1_), channel_id=1, source_target_pairs={{0,1},{1,0},{2,3},{3,2},{4,5},{5,4},{6,7},{7,6},{8,9},{9,8},{10,11... | collective-permute-start | bytes 1081352 | tf_op jit(solution)/shard_map/ppermute | solution.py:513
  292.0 3.7 %collective-permute-start.9 = (bf16[1,176,1024]{2,1,0:T(8,128)(2,1)S(1)}, bf16[1,176,1024]{2,1,0:T(8,128)(2,1)S(1)}, u32[]{:S(2)}, u32[]{:S(2)}) collective-permute-start(bf16[1,176,1024]{2,1,0:T(8,128)(2,1)S(1)} %collective-permute-done.2.refs_0_), channel_id=1, source_target_pairs={{0,1},{1,0},{2,3},{3,2},{4,5},{5,4},{6,7},{7,6},{8,9},{9,8},{10,11... | collective-permute-start | bytes 1081352 | tf_op jit(solution)/shard_map/ppermute | solution.py:513
  292.0 10.8 %collective-permute-start = (bf16[1,176,1024]{2,1,0:T(8,128)(2,1)S(1)}, bf16[1,176,1024]{2,1,0:T(8,128)(2,1)S(1)}, u32[]{:S(2)}, u32[]{:S(2)}) collective-permute-start(bf16[1,176,1024]{2,1,0:T(8,128)(2,1)S(1)} %copy-done.2), channel_id=1, source_target_pairs={{0,2},{1,3},{2,4},{3,5},{4,6},{5,7},{6,0},{7,1},{8,10},{9,11},{10,... | collective-permute-start | bytes 1081352 | tf_op jit(solution)/shard_map/ppermute | solution.py:505
  292.9 10.0 %collective-permute-start.1 = (bf16[1,176,1024]{2,1,0:T(8,128)(2,1)S(1)}, bf16[1,176,1024]{2,1,0:T(8,128)(2,1)S(1)}, u32[]{:S(2)}, u32[]{:S(2)}) collective-permute-start(bf16[1,176,1024]{2,1,0:T(8,128)(2,1)S(1)} %copy-done.1), channel_id=1, source_target_pairs={{0,6},{1,7},{2,0},{3,1},{4,2},{5,3},{6,4},{7,5},{8,14},{9,15},{10,... | collective-permute-start | bytes 1081352 | tf_op jit(solution)/shard_map/ppermute | solution.py:505
  302.9 2.6 collective-permute-start.11
  304.2 1.8 collective-permute-start.12

commit v5 on v4

--- a/solution.py
+++ b/solution.py
@@ -35,7 +35,16 @@
         self.members = [[p for p in range(self.count) if self.piece[p // self.layers] == k] for k in self.kinds]
 
         self.end = self.count - 1
-        self.groups = [*self.members[:-1], self.members[-1][:-1], [self.end]]
+        whole = [[(p, 0, k[0]) for p in m] for m, k in zip(self.members, self.kinds)]
+        rows = self.kinds[-1][0]
+        cut = (rows // GROUP + 1) // 2 * GROUP
+        self.groups = [*whole[:-1], whole[-1][:-1] + [(self.end, 0, cut)], [(self.end, cut, rows - cut)]]
+        self.late = [((sum(r for _, _, r in one), self.piece[one[0][0] // self.layers][1]), one) for one in self.groups]
+
+    def cuts(self):
+        n = self.kinds[-1][0] // GROUP
+        size = -(-n // 4)
+        return [(a, min(size, n - a)) for a in range(0, n, size)]
 
     def scratch(self, slots, dtype):
         return [pltpu.VMEM((len(m) * slots, *k), dtype) for m, k in zip(self.members, self.kinds)]
@@ -48,10 +57,10 @@
         kind, j = self.spot(p)
         return buffers[kind].at[j * slots + slot]
 
-    def rows(self, refs, p, block, half):
+    def rows(self, refs, p, block, half, first=0, size=None):
         w = p // self.layers
-        start = pl.multiple_of((block * 2 + half) * self.half[w], GROUP)
-        return refs[w].at[p % self.layers, pl.ds(start, self.half[w]), :]
+        start = pl.multiple_of((block * 2 + half) * self.half[w] + first, GROUP)
+        return refs[w].at[p % self.layers, pl.ds(start, self.half[w] if size is None else size), :]
 
     def own(self, refs, p, half):
         w = p // self.layers
@@ -60,16 +69,17 @@
 
 def exchange(places, count, *refs):
     nk = len(places.kinds)
-    names = (3, 3, 3, 3, 3, nk, nk, 1, 2 * len(places.groups) + 1, nk, nk, nk, nk, *(1,) * 10)
+    names = (3, 3, 3, 3, 3, nk, nk, 1, 2 * len(places.groups) + 1, nk, nk, nk, nk, *(1,) * 11)
     parts, i = [], 0
     for size in names:
         parts.append(refs[i : i + size])
         i += size
     g, w, m, v, whole, mm, vv, (factor_ref,), (*tails, last) = parts[:9]
     own, par, got, ww = parts[9:13]
-    (sq,), (own_sem,), (first_sem,), (par_recv,), (came_sem,), (pass_sem,), (all_sem,), (extra_send,), (extra_recv,), (end_recv,) = parts[13:]
+    (sq,), (own_sem,), (first_sem,), (par_recv,), (came_sem,), (pass_sem,), (all_sem,), (extra_send,), (extra_recv,), (end_recv,), (cut_sem,) = parts[13:]
 
     n, at, end = places.n, places.at, places.end
+    prev = end - 1
     chips = n // CORES
     me = lax.axis_index(AXIS)
     core, chip = lax.rem(me, CORES), lax.div(me, CORES)
@@ -106,6 +116,7 @@
     spots = range(places.count)
     steps = [(k + i, p) for k in (A, B, C) for p in spots for i in range(2)] + [(OWN + h, p) for p in spots for h in (1, 0)]
     groups = lambda p: places.half[p // places.layers] // GROUP
+    cuts = places.cuts()
     part = lambda ref, r: ref if r is None else ref.at[pl.ds(r * GROUP, GROUP), :]
 
     def load(t):
@@ -120,10 +131,15 @@
         src, dst = part(places.rows(g, p, away(to, 1 - core), half), r), part(at(par, 8, p, kind), r)
         return remote(src, dst, shared(SUM_GIVEN, p), recv, partner)
 
-    def send(kind, p, r=None):
+    def send(kind, p, r=None, rows=None):
         what, i = (SUM_A, SUM_B, SUM_C)[kind // 2], kind % 2
         recv = (came_sem.at[p, i], shared(B_CAME, p), pass_sem.at[p, i])[kind // 2]
-        return remote(part(at(own, 4, p, place(kind)[2]), r), part(at(got, 6, p, kind), r), shared(what, p), recv, beside[i])
+        src, dst = part(at(own, 4, p, place(kind)[2]), r), part(at(got, 6, p, kind), r)
+        if rows is not None:
+            first, size = cuts[rows]
+            src, dst = (ref.at[pl.ds(first * GROUP, size * GROUP), :] for ref in (src, dst))
+            recv = cut_sem.at[i, rows]
+        return remote(src, dst, shared(what, p), recv, beside[i])
 
     def start_load(t):
         if steps[t] in ((C, 0), (OWN + 1, 0)):
@@ -191,11 +207,21 @@
             if (kind, p) == (OWN + 1, 0):
                 for k in each:
                     all_of(B_CAME, k, got[k], 2 * len(places.members[k]))
-            if kind >= OWN:
+            if kind >= OWN and p != end:
                 send(C + 1 - (kind - OWN), p).wait_recv()
-            add_up(kind, p, 0, groups(p))
-            if kind < OWN:
+            if p != end or kind < C:
+                add_up(kind, p, 0, groups(p))
+            if p != end and kind < OWN or kind < C:
                 send(kind, p).start()
+            if p == end and C <= kind < OWN:
+                add_up(kind, p, 0, groups(p))
+                for r in range(len(cuts)):
+                    send(kind, p, rows=r).start()
+            if (kind, p) == (OWN, end):
+                for r, (first, size) in enumerate(cuts):
+                    for h in (1, 0):
+                        send(C + 1 - h, p, rows=r).wait_recv()
+                        add_up(OWN + h, p, first, first + size)
         if t + AHEAD < len(steps):
             start_load(t + AHEAD)
         if t == 2 * places.count:
@@ -231,7 +257,7 @@
         here = places.rows(whole, p, away(-sign[i], core), 1 - i)
         if p == end:
             return remote(here, last.at[i], extra_send.at[i], pass_sem.at[p, i], beside[i])
-        return remote(here, here, shared(SENT, p), pass_sem.at[p, i], beside[i])
+        return remote(here, last.at[4 + i] if p == prev else here, shared(SENT, p), pass_sem.at[p, i], beside[i])
 
     def onward_came(i, p):
         here = places.rows(whole, p, away(2, core), 1 - i)
@@ -278,8 +304,13 @@
                 ahead(1 - h, p, h).start()
             across(4 + h, p).start()
             pltpu.make_async_copy(at(ww, 2, p, h), places.rows(whole, p, me, h), shared(KEPT, p)).start()
-            k, j = next((k, one.index(p)) for k, one in enumerate(places.groups) if p in one)
-            pltpu.make_async_copy(at(ww, 2, p, h), tails[2 * k + h].at[j], shared(HANDED, p)).start()
+            for k, one in enumerate(places.groups):
+                start = 0
+                for q, first, size in one:
+                    if q == p:
+                        src, dst = at(ww, 2, p, h).at[pl.ds(first, size), :], tails[2 * k + h].at[pl.ds(start, size), :]
+                        pltpu.make_async_copy(src, dst, shared(HANDED, p)).start()
+                    start += size
     for p in spots:
         for i in range(2):
             ahead_came(i, p).wait_recv()
@@ -298,13 +329,14 @@
     for p in spots[:-1]:
         for i in range(2):
             onward_came(i, p).wait_recv()
-            across(2 + i, p).start()
+            if p != prev:
+                across(2 + i, p).start()
     for k in each:
         members = len(places.members[k])
         ends = 1 if k == kind_of(end) else 0
         all_of(SENT, k, own[k], 4 * members - 2 * ends)
-        all_of(ACROSS, k, par[k], 6 * members - 2 * ends)
-        all_of(ACROSS_CAME, k, par[k], 6 * members - 4 * ends)
+        all_of(ACROSS, k, par[k], 6 * members - 4 * ends)
+        all_of(ACROSS_CAME, k, par[k], 6 * members - 6 * ends)
         all_of(KEPT, k, ww[k], None)
         all_of(HANDED, k, ww[k], None)
     all_of(TOLD, 0, sq, n - 1)
@@ -329,8 +361,8 @@
     out = [pltpu.HBM(s, jnp.bfloat16) for s in shapes]
     out += places.scratch(2, jnp.float32) * 2
     out += [jax.ShapeDtypeStruct((8, 128), jnp.float32)]
-    out += [jax.ShapeDtypeStruct((len(one), *places.piece[one[0] // places.layers]), jnp.bfloat16) for one in places.groups for _ in range(2)]
-    out += [jax.ShapeDtypeStruct((4, *places.piece[-1]), jnp.bfloat16)]
+    out += [jax.ShapeDtypeStruct(shape, jnp.bfloat16) for shape, _ in places.late for _ in range(2)]
+    out += [jax.ShapeDtypeStruct((6, *places.piece[-1]), jnp.bfloat16)]
     dma = pltpu.SemaphoreType.DMA
     half, nk = jnp.bfloat16, len(places.kinds)
     scratch = [
@@ -338,7 +370,7 @@
         *places.scratch(2, half),
         pltpu.VMEM((n, 8, 128), jnp.float32),
         dma((RING,)), dma((2, places.half[0] // GROUP)), dma((2 * RING,)), dma((places.count, 2)), dma((places.count, 2)),
-        dma((15, nk)), dma((4,)), dma((2,)), dma((2,)),
+        dma((15, nk)), dma((4,)), dma((2,)), dma((2,)), dma((2, len(places.cuts()))),
     ]
     got = pl.pallas_call(
         functools.partial(exchange, places, count),
@@ -376,7 +408,7 @@
     items = []
     for p, h in pieces:
         for k in range(chips):
-            if p in tail and k == (1 if h else chips - 1) or p == places.end and k == 2:
+            if p in tail and k == (1 if h else chips - 1) or p >= places.end - 1 and k == 2:
                 continue
             items += [(p, h, k, c) for c in range(CORES)]
     turn, of_kind = [], [[] for _ in range(nk)]
@@ -449,39 +481,37 @@
 
 
 def place_late(places, spots, *refs):
-    k = len(spots)
+    k = max(one[0] for one in spots) + 1
     arrays, out, sem = refs[:k], refs[k + 3 : k + 6], refs[k + 6]
     chips = places.n // CORES
     me = lax.axis_index(AXIS)
     core, chip = lax.rem(me, CORES), lax.div(me, CORES)
     jobs = {}
-    for array, (only, pieces) in zip(arrays, spots):
-        for j, (p, h, away, which) in enumerate(pieces):
-            block = lax.rem(chip + (away + chips), chips) * CORES + (lax.rem(core + which[1], CORES) if which[0] else which[1])
-            mine = jobs.setdefault(only, [])
-            mine.append(pltpu.make_async_copy(array.at[j], places.rows(out, p, block, h), sem.at[sum(len(x) for x in jobs.values())]))
+    for number, (a, only, src, (p, first, size), h, away, (relative, which)) in enumerate(spots):
+        block = lax.rem(chip + (away + chips), chips) * CORES + (lax.rem(core + which, CORES) if relative else which)
+        src = arrays[a].at[src] if isinstance(src, int) else arrays[a].at[pl.ds(src[0], size), :]
+        jobs.setdefault(only, []).append(pltpu.make_async_copy(src, places.rows(out, p, block, h, first, size), sem.at[number]))
+
+    def run(copies):
+        for copy in copies:
+            copy.start()
+        for copy in copies:
+            copy.wait()
 
     for only, copies in jobs.items():
-
-        def run():
-            for copy in copies:
-                copy.start()
-            for copy in copies:
-                copy.wait()
-
-        run() if only is None else pl.when(core == only)(run)
+        run(copies) if only is None else pl.when(core == only)(functools.partial(run, copies))
 
 
 def place_all(places, spots, arrays, out):
     anywhere, vmem = pl.BlockSpec(memory_space=pl.ANY), pl.BlockSpec(memory_space=pltpu.VMEM)
-    k = len(spots)
+    k = len(arrays)
     return pl.pallas_call(
         functools.partial(place_late, places, spots),
         out_shape=[jax.ShapeDtypeStruct(w.shape, w.dtype) for w in out],
         in_specs=[vmem] * k + [anywhere] * 3,
         out_specs=[anywhere] * 3,
         input_output_aliases={k + j: j for j in range(3)},
-        scratch_shapes=[pltpu.SemaphoreType.DMA((sum(len(one) for _, one in spots),))],
+        scratch_shapes=[pltpu.SemaphoreType.DMA((len(spots),))],
         compiler_params=params(vmem_limit_bytes=16 * 1024 * 1024),
         cost_estimate=pl.CostEstimate(flops=10**7, bytes_accessed=sum(x.size for x in arrays) * 4, transcendentals=0),
         name="place_late",
@@ -506,16 +536,32 @@
         last_swapped = lax.ppermute(last, AXIS, swap)
         *out, m0, m1, m2, v0, v1, v2 = finish_all(places, tail, whole, mm, vv, m, v)
         own, other = (True, 0), (True, 1)
-        spots = lambda k, which: [(None, [(p, h, -1 if h == 0 else 1, which) for p in places.groups[k]]) for h in range(2)]
-        ends = [(places.end, 1 - i, 2, (False, c)) for c in (1, 0) for i in range(2)]
+
+        def spots(k, which, base):
+            found = []
+            for h in range(2):
+                start = 0
+                for p, first, size in places.groups[k]:
+                    found.append((base + h, None, (start,), (p, first, size), h, -1 if h == 0 else 1, which))
+                    start += size
+            return found
+
+        end, rows = places.end, places.kinds[-1][0]
+        far = lambda a, only, j, p, i, c: (a, only, j + i, (p, 0, rows), 1 - i, 2, (False, c))
+        ends = []
+        for i in range(2):
+            ends += [far(0, 1, 0, end, i, 1), far(0, 1, 2, end, i, 0), far(0, 1, 4, end - 1, i, 1), far(1, 1, 4, end - 1, i, 0)]
+            ends += [far(1, 0, 0, end, i, 1), far(1, 0, 2, end, i, 0), far(1, 0, 4, end - 1, i, 1), far(0, 0, 4, end - 1, i, 0)]
+        out = place_all(places, ends, [last, last_swapped], out)
+        crossed = {}
         for k in groups:
             here, out = lax.optimization_barrier((came[k], out))
-            swapped = [lax.ppermute(piece, AXIS, swap) for piece in here]
+            crossed[k] = [lax.ppermute(piece, AXIS, swap) for piece in here]
+            out = place_all(places, spots(k, own, 0), here, out)
             if k == 0:
-                out = place_all(places, [*spots(k, own), (1, ends), (0, ends)], [*here, last, last_swapped], out)
-            else:
-                out = place_all(places, spots(k, own), here, out)
-            out = place_all(places, spots(k, other), swapped, out)
+                out = place_all(places, spots(k, other, 0), crossed.pop(k), out)
+        work = [one for j, k in enumerate(crossed) for one in spots(k, other, 2 * j)]
+        out = place_all(places, work, [piece for one in crossed.values() for piece in one], out)
         return (*out, m0, m1, m2, v0, v1, v2)
 
     all_of, cut = P(None, None, None), P(None, AXIS, None)

time: 307 us -> 313 us (1.020)
  waiting for transfers between devices: 16.3 us -> 22.1 us
    ppermute x6, waiting for transfers between devices: 15.4 us -> 20.9 us  [step(): lax.ppermute(late[2 * k + h], AXIS, shift[h])]
  transfers between devices with their start and end apart: 13 -> 13, of which waited for: 5 -> 7; matrix products, arithmetic and copies ran while one was open for 0% -> 0% of each run, Pallas kernels for 10% -> 9%
where the time goes in v5:
time: 313 us
  Pallas kernels  277 us (88%)
  waiting for transfers between devices  22.1 us (7%)
  starting transfers between devices  12.6 us (4%)
    pallas_call x1, Pallas kernels, gather_new(): pl.pallas_call(functools.partial(exchange, places, count), out_shape=out,...  247 us
    pallas_call x1, Pallas kernels, finish_all(): pl.pallas_call(functools.partial(finish, places, tail), out_shape=[jax.Sh...  22.2 us
    ppermute x6, waiting for transfers between devices, step(): lax.ppermute(late[2 * k + h], AXIS, shift[h])  20.9 us
    ppermute x6, starting transfers between devices, step(): lax.ppermute(late[2 * k + h], AXIS, shift[h])  8.27 us
    pallas_call x6, Pallas kernels, place_all(): pl.pallas_call(functools.partial(place_late, places, spots), out_shape=[j...  7.88 us
  transfers between devices with their start and end apart: 13, of which 7 were waited for; matrix products, arithmetic and copies ran while one was open for 0% of the time, Pallas kernels for 9%

profile of v5, /device:TPU:113, one launch (start us, length us, event | category | flops | bytes accessed | tf_op | source)
XLA Modules:
  0.0 312.7 jit_solution(16451463273957124389)
XLA Ops:
  0.6 247.1 %exchange.1 = (bf16[2,1024,2816]{2,1,0:T(8,128)(2,1)}, bf16[2,1024,2816]{2,1,0:T(8,128)(2,1)}, bf16[2,2816,1024]{2,1,0:T(8,128)(2,1)}, f32[8,64,2816]{2,1,0:T(8,...) custom-call(bf16[2,1024,2816]{2,1,0:T(8,128)(2,1)} %bitcast.3, ...), custom_call_target="tpu_custom_call" | custom-call | tf_op jit(solution)/shard_map/exchange/pallas_call | solution.py:375
  247.7 0.1 collective-permute-start.4
  247.8 0.4 collective-permute-start.2
  248.2 2.4 collective-permute-start.3
  250.6 22.2 %finish.1 = (bf16[2,1024,2816]{2,1,0:T(8,128)(2,1)}, bf16[2,1024,2816]{2,1,0:T(8,128)(2,1)}, bf16[2,2816,1024]{2,1,0:T(8,128)(2,1)}, f32[2,128,2816]{2,1,0:T(8,1...) custom-call(bf16[2,1024,2816]{2,1,0:T(8,128)(2,1)} %get-tuple-elemen, ...), custom_call_target="tpu_custom_call" | custom-call | flops 1730150400 | bytes 86507520 | tf_op jit(solution)/shard_map/finish/pallas_call | solution.py:468
  272.8 0.0 collective-permute-done.4.refs_1_
  272.9 1.7 place_late.6
  274.6 7.5 %collective-permute-done.2.refs_0_ = bf16[256,2816]{1,0:T(8,128)(2,1)S(1)} collective-permute-done((bf16[256,2816]{1,0:T(8,128)(2,1)}, bf16[256,2816]{1,0:T(8,128)(2,1)S(1)}, u32[]{:S(2)}, u32[]{:S(2)}) %collective-permute-start.2) | collective-permute-done | bytes 1441824 | tf_op jit(solution)/shard_map/ppermute | solution.py:535
  282.1 0.0 collective-permute-done.3.refs_1_
  282.1 1.3 collective-permute-start.5
  283.3 0.0 collective-permute-start.6
  283.3 0.0 collective-permute-start
  283.3 2.8 collective-permute-start.1
  286.1 1.6 place_late.7
  287.7 0.0 collective-permute-done.5.refs_0_
  287.7 0.5 collective-permute-done.6.refs_1_
  288.2 1.6 place_late.8
  289.9 8.3 %collective-permute-done.refs_0_ = bf16[272,1024]{1,0:T(8,128)(2,1)S(1)} collective-permute-done((bf16[272,1024]{1,0:T(8,128)(2,1)S(1)}, bf16[272,1024]{1,0:T(8,128)(2,1)S(1)}, u32[]{:S(2)}, u32[]{:S(2)}) %collective-permute-start) | collective-permute-done | bytes 557088 | tf_op jit(solution)/shard_map/ppermute | solution.py:535
  298.2 1.4 collective-permute-start.7
  299.6 0.0 collective-permute-start.8
  299.6 2.8 collective-permute-start.10
  302.4 1.0 place_late.9
  303.4 2.0 collective-permute-done.10.refs_1_
  305.4 3.1 %collective-permute-done.9.refs_0_ = bf16[80,1024]{1,0:T(8,128)(2,1)S(1)} collective-permute-done((bf16[80,1024]{1,0:T(8,128)(2,1)S(1)}, bf16[80,1024]{1,0:T(8,128)(2,1)S(1)}, u32[]{:S(2)}, u32[]{:S(2)}) %collective-permute-start.9) | collective-permute-done | bytes 163872 | tf_op jit(solution)/shard_map/ppermute | solution.py:535
  308.5 1.6 collective-permute-start.11
  310.2 0.0 collective-permute-start.12
  310.2 0.7 place_late.10
  310.9 0.3 collective-permute-done.11.refs_2_
  311.2 0.4 collective-permute-done.12.refs_3_
  311.6 0.0 collective-permute-done.7.refs_0_
  311.6 0.0 collective-permute-done.8.refs_1_
  311.6 1.1 place_late.11
  (12 shorter events, 0.0 us)
Async XLA Ops:
  247.7 25.1 %collective-permute-start.4 = (bf16[6,176,1024]{2,1,0:T(8,128)(2,1)}, bf16[6,176,1024]{2,1,0:T(8,128)(2,1)S(1)}, u32[]{:S(2)}, u32[]{:S(2)}) collective-permute-start(bf16[6,176,1024]{2,1,0:T(8,128)(2,1)} %get-tuple-element.69.refs_0_), channel_id=1, source_target_pairs={{0,1},{1,0},{2,3},{3,2},{4,5},{5,4},{6,7},{7,6},{8,9},{9,8},{10,11... | collective-permute-start | bytes 6488072 | tf_op jit(solution)/shard_map/ppermute | solution.py:536
  247.8 34.2 %collective-permute-start.2 = (bf16[256,2816]{1,0:T(8,128)(2,1)}, bf16[256,2816]{1,0:T(8,128)(2,1)S(1)}, u32[]{:S(2)}, u32[]{:S(2)}) collective-permute-start(bf16[256,2816]{1,0:T(8,128)(2,1)} %get-tuple-element.67), channel_id=1, source_target_pairs={{0,2},{1,3},{2,4},{3,5},{4,6},{5,7},{6,0},{7,1},{8,10},{9,11},{10,... | collective-permute-start | bytes 4325384 | tf_op jit(solution)/shard_map/ppermute | solution.py:535
  248.2 33.8 %collective-permute-start.3 = (bf16[256,2816]{1,0:T(8,128)(2,1)}, bf16[256,2816]{1,0:T(8,128)(2,1)S(1)}, u32[]{:S(2)}, u32[]{:S(2)}) collective-permute-start(bf16[256,2816]{1,0:T(8,128)(2,1)} %get-tuple-element.68), channel_id=1, source_target_pairs={{0,6},{1,7},{2,0},{3,1},{4,2},{5,3},{6,4},{7,5},{8,14},{9,15},{10,... | collective-permute-start | bytes 4325384 | tf_op jit(solution)/shard_map/ppermute | solution.py:535
  250.6 22.3 %copy-start = (bf16[6,176,1024]{2,1,0:T(8,128)(2,1)S(1)}, bf16[6,176,1024]{2,1,0:T(8,128)(2,1)}, u32[]{:S(2)}) copy-start(bf16[6,176,1024]{2,1,0:T(8,128)(2,1)} %get-tuple-element.69.refs_0_) | copy-start | bytes 6488068
  272.8 10.5 %copy-start.2 = (bf16[272,1024]{1,0:T(8,128)(2,1)S(1)}, bf16[272,1024]{1,0:T(8,128)(2,1)}, u32[]{:S(2)}) copy-start(bf16[272,1024]{1,0:T(8,128)(2,1)} %get-tuple-element.65) | copy-start | bytes 1671172
  272.9 10.5 %copy-start.1 = (bf16[272,1024]{1,0:T(8,128)(2,1)S(1)}, bf16[272,1024]{1,0:T(8,128)(2,1)}, u32[]{:S(2)}) copy-start(bf16[272,1024]{1,0:T(8,128)(2,1)} %get-tuple-element.66) | copy-start | bytes 1671172
  282.1 5.7 %collective-permute-start.5 = (bf16[256,2816]{1,0:T(8,128)(2,1)S(1)}, bf16[256,2816]{1,0:T(8,128)(2,1)S(1)}, u32[]{:S(2)}, u32[]{:S(2)}) collective-permute-start(bf16[256,2816]{1,0:T(8,128)(2,1)S(1)} %collective-permute-done.2.refs_0_), channel_id=1, source_target_pairs={{0,1},{1,0},{2,3},{3,2},{4,5},{5,4},{6,7},{7,6},{8,9},{9,8},{10,11... | collective-permute-start | bytes 4325384 | tf_op jit(solution)/shard_map/ppermute | solution.py:559
  283.3 4.9 %collective-permute-start.6 = (bf16[256,2816]{1,0:T(8,128)(2,1)S(1)}, bf16[256,2816]{1,0:T(8,128)(2,1)S(1)}, u32[]{:S(2)}, u32[]{:S(2)}) collective-permute-start(bf16[256,2816]{1,0:T(8,128)(2,1)S(1)} %collective-permute-done.3.refs_1_), channel_id=1, source_target_pairs={{0,1},{1,0},{2,3},{3,2},{4,5},{5,4},{6,7},{7,6},{8,9},{9,8},{10,11... | collective-permute-start | bytes 4325384 | tf_op jit(solution)/shard_map/ppermute | solution.py:559
  283.3 14.9 %collective-permute-start = (bf16[272,1024]{1,0:T(8,128)(2,1)S(1)}, bf16[272,1024]{1,0:T(8,128)(2,1)S(1)}, u32[]{:S(2)}, u32[]{:S(2)}) collective-permute-start(bf16[272,1024]{1,0:T(8,128)(2,1)S(1)} %copy-done.2), channel_id=1, source_target_pairs={{0,2},{1,3},{2,4},{3,5},{4,6},{5,7},{6,0},{7,1},{8,10},{9,11},{10,... | collective-permute-start | bytes 1671176 | tf_op jit(solution)/shard_map/ppermute | solution.py:535
  283.3 14.9 %collective-permute-start.1 = (bf16[272,1024]{1,0:T(8,128)(2,1)S(1)}, bf16[272,1024]{1,0:T(8,128)(2,1)S(1)}, u32[]{:S(2)}, u32[]{:S(2)}) collective-permute-start(bf16[272,1024]{1,0:T(8,128)(2,1)S(1)} %copy-done.1), channel_id=1, source_target_pairs={{0,6},{1,7},{2,0},{3,1},{4,2},{5,3},{6,4},{7,5},{8,14},{9,15},{10,... | collective-permute-start | bytes 1671176 | tf_op jit(solution)/shard_map/ppermute | solution.py:535
  288.2 11.4 %copy-start.4 = (bf16[80,1024]{1,0:T(8,128)(2,1)S(1)}, bf16[80,1024]{1,0:T(8,128)(2,1)}, u32[]{:S(2)}) copy-start(bf16[80,1024]{1,0:T(8,128)(2,1)} %get-tuple-element.97) | copy-start | bytes 491524
  288.2 14.1 %copy-start.3 = (bf16[80,1024]{1,0:T(8,128)(2,1)S(1)}, bf16[80,1024]{1,0:T(8,128)(2,1)}, u32[]{:S(2)}) copy-start(bf16[80,1024]{1,0:T(8,128)(2,1)} %get-tuple-element.96) | copy-start | bytes 491524
  298.2 13.4 %collective-permute-start.7 = (bf16[272,1024]{1,0:T(8,128)(2,1)S(1)}, bf16[272,1024]{1,0:T(8,128)(2,1)S(1)}, u32[]{:S(2)}, u32[]{:S(2)}) collective-permute-start(bf16[272,1024]{1,0:T(8,128)(2,1)S(1)} %collective-permute-done.refs_0_), channel_id=1, source_target_pairs={{0,1},{1,0},{2,3},{3,2},{4,5},{5,4},{6,7},{7,6},{8,9},{9,8},{10,11... | collective-permute-start | bytes 1671176 | tf_op jit(solution)/shard_map/ppermute | solution.py:559
  299.6 12.0 %collective-permute-start.8 = (bf16[272,1024]{1,0:T(8,128)(2,1)S(1)}, bf16[272,1024]{1,0:T(8,128)(2,1)S(1)}, u32[]{:S(2)}, u32[]{:S(2)}) collective-permute-start(bf16[272,1024]{1,0:T(8,128)(2,1)S(1)} %collective-permute-done.1.refs_1_), channel_id=1, source_target_pairs={{0,1},{1,0},{2,3},{3,2},{4,5},{5,4},{6,7},{7,6},{8,9},{9,8},{10,11... | collective-permute-start | bytes 1671176 | tf_op jit(solution)/shard_map/ppermute | solution.py:559
  299.6 5.8 %collective-permute-start.10 = (bf16[80,1024]{1,0:T(8,128)(2,1)S(1)}, bf16[80,1024]{1,0:T(8,128)(2,1)S(1)}, u32[]{:S(2)}, u32[]{:S(2)}) collective-permute-start(bf16[80,1024]{1,0:T(8,128)(2,1)S(1)} %copy-done.4), channel_id=1, source_target_pairs={{0,6},{1,7},{2,0},{3,1},{4,2},{5,3},{6,4},{7,5},{8,14},{9,15},{10,... | collective-permute-start | bytes 491528 | tf_op jit(solution)/shard_map/ppermute | solution.py:535
  302.4 6.2 %collective-permute-start.9 = (bf16[80,1024]{1,0:T(8,128)(2,1)S(1)}, bf16[80,1024]{1,0:T(8,128)(2,1)S(1)}, u32[]{:S(2)}, u32[]{:S(2)}) collective-permute-start(bf16[80,1024]{1,0:T(8,128)(2,1)S(1)} %copy-done.3), channel_id=1, source_target_pairs={{0,2},{1,3},{2,4},{3,5},{4,6},{5,7},{6,0},{7,1},{8,10},{9,11},{10,... | collective-permute-start | bytes 491528 | tf_op jit(solution)/shard_map/ppermute | solution.py:535
  308.5 2.7 collective-permute-start.11
  310.2 1.4 collective-permute-start.12

commit v6 on v5

--- a/solution.py
+++ b/solution.py
@@ -10,7 +10,7 @@
 
 AXIS = "dp"
 CORES = 2
-AHEAD = 6
+AHEAD = 4
 GROUP = 16
 RING = 8
 SLOTS, DEPTH = 16, 8
@@ -43,7 +43,7 @@
 
     def cuts(self):
         n = self.kinds[-1][0] // GROUP
-        size = -(-n // 4)
+        size = -(-n // 8)
         return [(a, min(size, n - a)) for a in range(0, n, size)]
 
     def scratch(self, slots, dtype):
@@ -176,18 +176,19 @@
         else:
             sq[me] = lax.fori_loop(first, last, body, sq[me])
 
-    for t in range(AHEAD):
+    barrier = pltpu.get_barrier_semaphore()
+    for device in (*beside, partner):
+        pl.semaphore_signal(barrier, inc=1, device_id={AXIS: device}, device_id_type=pl.DeviceIdType.MESH)
+    for t in range(2):
         start_load(t)
-    barrier = pltpu.get_barrier_semaphore()
-    for device in (partner, *beside):
-        pl.semaphore_signal(barrier, inc=1, device_id={AXIS: device}, device_id_type=pl.DeviceIdType.MESH)
+    sq[me] = jnp.zeros(sq.shape[1:], jnp.float32)
     pl.semaphore_wait(barrier, 3)
     for r in range(groups(0)):
         for t in range(2):
             give(t, r).start()
     for t in range(2, AHEAD):
         give(t).start()
-    sq[me] = jnp.zeros(sq.shape[1:], jnp.float32)
+        start_load(t)
 
     for r in range(groups(0)):
         for t in range(2):
@@ -231,11 +232,9 @@
                     pltpu.make_async_copy(places.own(v, q, h), at(vv, 2, q, h), shared(V, q)).start()
                     pltpu.make_async_copy(places.rows(w, q, me, h), at(ww, 2, q, h), shared(W, q)).start()
 
-    for o in range(1, n):
+    for o in sorted(range(1, n), key=lambda o: -min(o, n - o)):
         remote(sq.at[me], sq.at[me], all_sem.at[TOLD, 0], all_sem.at[HEARD, 0], lax.rem(me + o, n)).start()
     for k in each:
-        all_of(SUM_C, k, own[k], 2 * len(places.members[k]))
-        all_of(SUM_GIVEN, k, par[k], None)
         for what, buffers in ((M, mm), (V, vv), (W, ww)):
             all_of(what, k, buffers[k], None)
     all_of(HEARD, 0, sq, n - 1)
@@ -334,6 +333,8 @@
     for k in each:
         members = len(places.members[k])
         ends = 1 if k == kind_of(end) else 0
+        all_of(SUM_C, k, own[k], 2 * members)
+        all_of(SUM_GIVEN, k, par[k], None)
         all_of(SENT, k, own[k], 4 * members - 2 * ends)
         all_of(ACROSS, k, par[k], 6 * members - 4 * ends)
         all_of(ACROSS_CAME, k, par[k], 6 * members - 6 * ends)

time: 313 us -> 313 us (level)
  no operation moved by 1% of the time
where the time goes in v6:
time: 313 us
  Pallas kernels  277 us (88%)
  waiting for transfers between devices  22.1 us (7%)
  starting transfers between devices  12.6 us (4%)
    pallas_call x1, Pallas kernels, gather_new(): pl.pallas_call(functools.partial(exchange, places, count), out_shape=out,...  247 us
    pallas_call x1, Pallas kernels, finish_all(): pl.pallas_call(functools.partial(finish, places, tail), out_shape=[jax.Sh...  22.2 us
    ppermute x6, waiting for transfers between devices, step(): lax.ppermute(late[2 * k + h], AXIS, shift[h])  20.9 us
    ppermute x6, starting transfers between devices, step(): lax.ppermute(late[2 * k + h], AXIS, shift[h])  8.27 us
    pallas_call x6, Pallas kernels, place_all(): pl.pallas_call(functools.partial(place_late, places, spots), out_shape=[j...  7.88 us
  transfers between devices with their start and end apart: 13, of which 7 were waited for; matrix products, arithmetic and copies ran while one was open for 0% of the time, Pallas kernels for 9%

profile of v6, /device:TPU:113, one launch (start us, length us, event | category | flops | bytes accessed | tf_op | source)
XLA Modules:
  0.0 312.6 jit_solution(15404806194919837320)
XLA Ops:
  0.6 246.9 %exchange.1 = (bf16[2,1024,2816]{2,1,0:T(8,128)(2,1)}, bf16[2,1024,2816]{2,1,0:T(8,128)(2,1)}, bf16[2,2816,1024]{2,1,0:T(8,128)(2,1)}, f32[8,64,2816]{2,1,0:T(8,...) custom-call(bf16[2,1024,2816]{2,1,0:T(8,128)(2,1)} %bitcast.3, ...), custom_call_target="tpu_custom_call" | custom-call | tf_op jit(solution)/shard_map/exchange/pallas_call | solution.py:376
  247.6 0.1 collective-permute-start.4
  247.7 0.2 collective-permute-start.2
  247.9 2.6 collective-permute-start.3
  250.4 22.2 %finish.1 = (bf16[2,1024,2816]{2,1,0:T(8,128)(2,1)}, bf16[2,1024,2816]{2,1,0:T(8,128)(2,1)}, bf16[2,2816,1024]{2,1,0:T(8,128)(2,1)}, f32[2,128,2816]{2,1,0:T(8,1...) custom-call(bf16[2,1024,2816]{2,1,0:T(8,128)(2,1)} %get-tuple-elemen, ...), custom_call_target="tpu_custom_call" | custom-call | flops 1730150400 | bytes 86507520 | tf_op jit(solution)/shard_map/finish/pallas_call | solution.py:469
  272.7 0.0 collective-permute-done.4.refs_1_
  272.7 1.7 place_late.6
  274.5 7.5 %collective-permute-done.2.refs_0_ = bf16[256,2816]{1,0:T(8,128)(2,1)S(1)} collective-permute-done((bf16[256,2816]{1,0:T(8,128)(2,1)}, bf16[256,2816]{1,0:T(8,128)(2,1)S(1)}, u32[]{:S(2)}, u32[]{:S(2)}) %collective-permute-start.2) | collective-permute-done | bytes 1441824 | tf_op jit(solution)/shard_map/ppermute | solution.py:536
  281.9 0.0 collective-permute-done.3.refs_1_
  281.9 1.3 collective-permute-start.5
  283.2 0.0 collective-permute-start.6
  283.2 0.0 collective-permute-start
  283.2 2.8 collective-permute-start.1
  286.0 1.6 place_late.7
  287.6 0.0 collective-permute-done.5.refs_0_
  287.6 0.5 collective-permute-done.6.refs_1_
  288.1 1.6 place_late.8
  289.8 8.3 %collective-permute-done.refs_0_ = bf16[272,1024]{1,0:T(8,128)(2,1)S(1)} collective-permute-done((bf16[272,1024]{1,0:T(8,128)(2,1)S(1)}, bf16[272,1024]{1,0:T(8,128)(2,1)S(1)}, u32[]{:S(2)}, u32[]{:S(2)}) %collective-permute-start) | collective-permute-done | bytes 557088 | tf_op jit(solution)/shard_map/ppermute | solution.py:536
  298.1 0.0 collective-permute-done.1.refs_1_
  298.1 1.4 collective-permute-start.7
  299.5 0.0 collective-permute-start.8
  299.5 2.8 collective-permute-start.10
  302.2 1.0 place_late.9
  303.3 2.0 collective-permute-done.10.refs_1_
  305.3 3.1 %collective-permute-done.9.refs_0_ = bf16[80,1024]{1,0:T(8,128)(2,1)S(1)} collective-permute-done((bf16[80,1024]{1,0:T(8,128)(2,1)S(1)}, bf16[80,1024]{1,0:T(8,128)(2,1)S(1)}, u32[]{:S(2)}, u32[]{:S(2)}) %collective-permute-start.9) | collective-permute-done | bytes 163872 | tf_op jit(solution)/shard_map/ppermute | solution.py:536
  308.4 1.6 collective-permute-start.11
  310.1 0.0 collective-permute-start.12
  310.1 0.7 place_late.10
  310.8 0.3 collective-permute-done.11.refs_2_
  311.1 0.4 collective-permute-done.12.refs_3_
  311.5 0.0 collective-permute-done.7.refs_0_
  311.5 1.1 place_late.11
  (12 shorter events, 0.0 us)
Async XLA Ops:
  247.6 25.1 %collective-permute-start.4 = (bf16[6,176,1024]{2,1,0:T(8,128)(2,1)}, bf16[6,176,1024]{2,1,0:T(8,128)(2,1)S(1)}, u32[]{:S(2)}, u32[]{:S(2)}) collective-permute-start(bf16[6,176,1024]{2,1,0:T(8,128)(2,1)} %get-tuple-element.69.refs_0_), channel_id=1, source_target_pairs={{0,1},{1,0},{2,3},{3,2},{4,5},{5,4},{6,7},{7,6},{8,9},{9,8},{10,11... | collective-permute-start | bytes 6488072 | tf_op jit(solution)/shard_map/ppermute | solution.py:537
  247.7 34.2 %collective-permute-start.2 = (bf16[256,2816]{1,0:T(8,128)(2,1)}, bf16[256,2816]{1,0:T(8,128)(2,1)S(1)}, u32[]{:S(2)}, u32[]{:S(2)}) collective-permute-start(bf16[256,2816]{1,0:T(8,128)(2,1)} %get-tuple-element.67), channel_id=1, source_target_pairs={{0,2},{1,3},{2,4},{3,5},{4,6},{5,7},{6,0},{7,1},{8,10},{9,11},{10,... | collective-permute-start | bytes 4325384 | tf_op jit(solution)/shard_map/ppermute | solution.py:536
  247.9 34.1 %collective-permute-start.3 = (bf16[256,2816]{1,0:T(8,128)(2,1)}, bf16[256,2816]{1,0:T(8,128)(2,1)S(1)}, u32[]{:S(2)}, u32[]{:S(2)}) collective-permute-start(bf16[256,2816]{1,0:T(8,128)(2,1)} %get-tuple-element.68), channel_id=1, source_target_pairs={{0,6},{1,7},{2,0},{3,1},{4,2},{5,3},{6,4},{7,5},{8,14},{9,15},{10,... | collective-permute-start | bytes 4325384 | tf_op jit(solution)/shard_map/ppermute | solution.py:536
  250.4 22.3 %copy-start = (bf16[6,176,1024]{2,1,0:T(8,128)(2,1)S(1)}, bf16[6,176,1024]{2,1,0:T(8,128)(2,1)}, u32[]{:S(2)}) copy-start(bf16[6,176,1024]{2,1,0:T(8,128)(2,1)} %get-tuple-element.69.refs_0_) | copy-start | bytes 6488068
  272.7 10.5 %copy-start.2 = (bf16[272,1024]{1,0:T(8,128)(2,1)S(1)}, bf16[272,1024]{1,0:T(8,128)(2,1)}, u32[]{:S(2)}) copy-start(bf16[272,1024]{1,0:T(8,128)(2,1)} %get-tuple-element.65) | copy-start | bytes 1671172
  272.7 10.5 %copy-start.1 = (bf16[272,1024]{1,0:T(8,128)(2,1)S(1)}, bf16[272,1024]{1,0:T(8,128)(2,1)}, u32[]{:S(2)}) copy-start(bf16[272,1024]{1,0:T(8,128)(2,1)} %get-tuple-element.66) | copy-start | bytes 1671172
  281.9 5.7 %collective-permute-start.5 = (bf16[256,2816]{1,0:T(8,128)(2,1)S(1)}, bf16[256,2816]{1,0:T(8,128)(2,1)S(1)}, u32[]{:S(2)}, u32[]{:S(2)}) collective-permute-start(bf16[256,2816]{1,0:T(8,128)(2,1)S(1)} %collective-permute-done.2.refs_0_), channel_id=1, source_target_pairs={{0,1},{1,0},{2,3},{3,2},{4,5},{5,4},{6,7},{7,6},{8,9},{9,8},{10,11... | collective-permute-start | bytes 4325384 | tf_op jit(solution)/shard_map/ppermute | solution.py:560
  283.2 4.9 %collective-permute-start.6 = (bf16[256,2816]{1,0:T(8,128)(2,1)S(1)}, bf16[256,2816]{1,0:T(8,128)(2,1)S(1)}, u32[]{:S(2)}, u32[]{:S(2)}) collective-permute-start(bf16[256,2816]{1,0:T(8,128)(2,1)S(1)} %collective-permute-done.3.refs_1_), channel_id=1, source_target_pairs={{0,1},{1,0},{2,3},{3,2},{4,5},{5,4},{6,7},{7,6},{8,9},{9,8},{10,11... | collective-permute-start | bytes 4325384 | tf_op jit(solution)/shard_map/ppermute | solution.py:560
  283.2 14.9 %collective-permute-start = (bf16[272,1024]{1,0:T(8,128)(2,1)S(1)}, bf16[272,1024]{1,0:T(8,128)(2,1)S(1)}, u32[]{:S(2)}, u32[]{:S(2)}) collective-permute-start(bf16[272,1024]{1,0:T(8,128)(2,1)S(1)} %copy-done.2), channel_id=1, source_target_pairs={{0,2},{1,3},{2,4},{3,5},{4,6},{5,7},{6,0},{7,1},{8,10},{9,11},{10,... | collective-permute-start | bytes 1671176 | tf_op jit(solution)/shard_map/ppermute | solution.py:536
  283.2 14.9 %collective-permute-start.1 = (bf16[272,1024]{1,0:T(8,128)(2,1)S(1)}, bf16[272,1024]{1,0:T(8,128)(2,1)S(1)}, u32[]{:S(2)}, u32[]{:S(2)}) collective-permute-start(bf16[272,1024]{1,0:T(8,128)(2,1)S(1)} %copy-done.1), channel_id=1, source_target_pairs={{0,6},{1,7},{2,0},{3,1},{4,2},{5,3},{6,4},{7,5},{8,14},{9,15},{10,... | collective-permute-start | bytes 1671176 | tf_op jit(solution)/shard_map/ppermute | solution.py:536
  288.1 11.4 %copy-start.4 = (bf16[80,1024]{1,0:T(8,128)(2,1)S(1)}, bf16[80,1024]{1,0:T(8,128)(2,1)}, u32[]{:S(2)}) copy-start(bf16[80,1024]{1,0:T(8,128)(2,1)} %get-tuple-element.97) | copy-start | bytes 491524
  288.1 14.1 %copy-start.3 = (bf16[80,1024]{1,0:T(8,128)(2,1)S(1)}, bf16[80,1024]{1,0:T(8,128)(2,1)}, u32[]{:S(2)}) copy-start(bf16[80,1024]{1,0:T(8,128)(2,1)} %get-tuple-element.96) | copy-start | bytes 491524
  298.1 13.4 %collective-permute-start.7 = (bf16[272,1024]{1,0:T(8,128)(2,1)S(1)}, bf16[272,1024]{1,0:T(8,128)(2,1)S(1)}, u32[]{:S(2)}, u32[]{:S(2)}) collective-permute-start(bf16[272,1024]{1,0:T(8,128)(2,1)S(1)} %collective-permute-done.refs_0_), channel_id=1, source_target_pairs={{0,1},{1,0},{2,3},{3,2},{4,5},{5,4},{6,7},{7,6},{8,9},{9,8},{10,11... | collective-permute-start | bytes 1671176 | tf_op jit(solution)/shard_map/ppermute | solution.py:560
  299.5 12.0 %collective-permute-start.8 = (bf16[272,1024]{1,0:T(8,128)(2,1)S(1)}, bf16[272,1024]{1,0:T(8,128)(2,1)S(1)}, u32[]{:S(2)}, u32[]{:S(2)}) collective-permute-start(bf16[272,1024]{1,0:T(8,128)(2,1)S(1)} %collective-permute-done.1.refs_1_), channel_id=1, source_target_pairs={{0,1},{1,0},{2,3},{3,2},{4,5},{5,4},{6,7},{7,6},{8,9},{9,8},{10,11... | collective-permute-start | bytes 1671176 | tf_op jit(solution)/shard_map/ppermute | solution.py:560
  299.5 5.8 %collective-permute-start.10 = (bf16[80,1024]{1,0:T(8,128)(2,1)S(1)}, bf16[80,1024]{1,0:T(8,128)(2,1)S(1)}, u32[]{:S(2)}, u32[]{:S(2)}) collective-permute-start(bf16[80,1024]{1,0:T(8,128)(2,1)S(1)} %copy-done.4), channel_id=1, source_target_pairs={{0,6},{1,7},{2,0},{3,1},{4,2},{5,3},{6,4},{7,5},{8,14},{9,15},{10,... | collective-permute-start | bytes 491528 | tf_op jit(solution)/shard_map/ppermute | solution.py:536
  302.2 6.2 %collective-permute-start.9 = (bf16[80,1024]{1,0:T(8,128)(2,1)S(1)}, bf16[80,1024]{1,0:T(8,128)(2,1)S(1)}, u32[]{:S(2)}, u32[]{:S(2)}) collective-permute-start(bf16[80,1024]{1,0:T(8,128)(2,1)S(1)} %copy-done.3), channel_id=1, source_target_pairs={{0,2},{1,3},{2,4},{3,5},{4,6},{5,7},{6,0},{7,1},{8,10},{9,11},{10,... | collective-permute-start | bytes 491528 | tf_op jit(solution)/shard_map/ppermute | solution.py:536
  308.4 2.7 collective-permute-start.11
  310.1 1.4 collective-permute-start.12
